TPU v7x, 32 devices: a whole 2x2x4 slice. The times are simulated.
32 devices in a mesh: groups: 2 (over y), expert: 16 (over z, x, core).
Axes of the slice: x: 2, y: 2, z: 4, core: 2. Of those that a mesh axis runs over, the one named last changes fastest.
Arguments:
- tokens: bfloat16 [512, 3584], P(('groups', 'expert')), parts along dimension 0, may hold values from -6 to 6
- live_counts: int32 [32], P(('groups', 'expert')), parts along dimension 0, may hold values from 8 to 16, as said below
- expert_ids: int32 [512, 4], P(('groups', 'expert')), parts along dimension 0, may hold values from 0 to 7, all different within a row; in each aligned block of 16 rows (0 to 15, 16 to 31, ...) at most 16 rows name the same one
- gate_scores: float32 [512, 4], P(('groups', 'expert')), parts along dimension 0, may hold values from 0.1 to 1
- gate_weight: bfloat16 [16, 3584, 512], P('expert'), may hold values from -0.09375 to 0.09375
- up_weight: bfloat16 [16, 3584, 512], P('expert'), may hold values from -0.09375 to 0.09375
- down_weight: bfloat16 [16, 512, 3584], P('expert'), may hold values from -0.1875 to 0.1875
Outputs:
- moe_out: bfloat16 [512, 3584], P(('groups', 'expert')), parts along dimension 0
There are 2 independent parts, one for each index of `groups`. A program takes and returns all parts, laid end to end along the dimension named above; an argument that names none is the same for every part. Nothing has to cross between parts.
Inputs may be any that keep to these rules, and one draw needn't show every extreme that they name: `expert_ids`: A row names 4 different experts. In each device's aligned block of 16 rows no expert is named by more than 16 rows, a bound that some block reaches. `live_counts`: some device has all 16 slots live.
All inputs are finite; a program needn't handle non-finite values.
Results may differ from a plain program's by a relative error of at most 0.0068.
Values may be sent and summed in bfloat16 or wider, within the bound.
No kernel may reach another device: no remote copies, remote signals or barrier semaphores. Data moves between devices by JAX's collectives and lax.ppermute only.
A program may use at most 64 MiB of HBM per device.

v0:
```python
import jax
import jax.numpy as jnp
from jax import lax
from jax.sharding import PartitionSpec as P


def partner_2(block, axis, apart):
    count = lax.axis_size(axis)
    route = []
    for low in range(count):
        high = low | 1 << apart
        if high != low and high < count:
            route += [(low, high), (high, low)]
    return lax.ppermute(block, axis, route)


def expert_rows(slot_rows, gate_weight, up_weight, down_weight):
    model_width = slot_rows.shape[-1]
    flat_rows = slot_rows.reshape(-1, model_width)
    gate_act = jnp.dot(flat_rows, gate_weight[0], preferred_element_type=jnp.float32)
    up_act = jnp.dot(flat_rows, up_weight[0], preferred_element_type=jnp.float32)
    hidden = (jax.nn.silu(gate_act) * up_act).astype(jnp.bfloat16)
    partial_value = jnp.dot(hidden, down_weight[0], preferred_element_type=jnp.float32)
    return partial_value.reshape(slot_rows.shape)


def shards(tokens, live_counts, expert_ids, gate_scores, gate_weight, up_weight, down_weight):
    tok_dev, model_width = tokens.shape
    top_count = expert_ids.shape[1]
    devices = lax.axis_size("expert")
    experts = devices // 2
    capacity = 2 * tok_dev * top_count // experts
    half_width = model_width // 2
    parity = lax.axis_index("expert") % 2
    flat_ids = expert_ids.reshape(-1)
    onehot = (flat_ids[:, None] == jnp.arange(experts, dtype=jnp.int32)[None, :]).astype(jnp.int32)
    earlier = jnp.cumsum(onehot, axis=0) - onehot
    slot_index = jnp.sum(earlier * onehot, axis=1)
    target = flat_ids * capacity + slot_index
    placing = (jnp.arange(experts * capacity, dtype=jnp.int32)[:, None] == target[None, :]).astype(
        jnp.int32
    )
    placing = (
        placing.reshape(experts * capacity, tok_dev, top_count).sum(axis=2).astype(jnp.bfloat16)
    )
    packed = jnp.dot(placing, tokens, preferred_element_type=jnp.float32).astype(jnp.bfloat16)
    outgoing = packed.reshape(devices, capacity // 2, model_width)
    slot_rows = lax.all_to_all(outgoing, "expert", split_axis=0, concat_axis=0, tiled=True)
    partner = partner_2(slot_rows, "expert", 0)
    count = slot_rows.shape[1]
    run_slot_rows = jnp.concatenate([slot_rows, partner], axis=1)
    paired = expert_rows(run_slot_rows, gate_weight, up_weight, down_weight)
    own_part = paired[:, :count]
    partner_part = paired[:, count:]
    lower_half = jnp.where(parity == 0, own_part, partner_part)
    second = jnp.where(parity == 0, partner_part, own_part)
    stacked = jnp.stack([lower_half, second], axis=1)
    partial_value = stacked.reshape(devices, capacity, model_width)
    partner_sum = partner_2(partial_value, "expert", 0)
    summed = partial_value + partner_sum
    own_part = lax.dynamic_slice_in_dim(summed, parity * half_width, half_width, 2).astype(
        jnp.bfloat16
    )
    returned = lax.all_to_all(own_part, "expert", split_axis=0, concat_axis=0, tiled=True)
    returned = returned.reshape(experts, 2, capacity, half_width)
    picked = returned[flat_ids, :, slot_index, :]
    picked = picked.reshape(tok_dev, top_count, model_width).astype(jnp.float32)
    weighted = jnp.sum(picked * gate_scores[:, :, None], axis=1)
    live_mask = jnp.arange(tok_dev, dtype=jnp.int32) < live_counts[0]
    return jnp.where(live_mask[:, None], weighted, jnp.zeros_like(weighted)).astype(jnp.bfloat16)


def solution(mesh):
    in_specs = (
        P(("groups", "expert"), None),
        P(("groups", "expert")),
        P(("groups", "expert"), None),
        P(("groups", "expert"), None),
        P("expert", None, None),
        P("expert", None, None),
        P("expert", None, None),
    )
    out_specs = P(("groups", "expert"), None)
    return jax.shard_map(shards, mesh=mesh, in_specs=in_specs, out_specs=out_specs, check_vma=False)
```

profile of v0, /device:TPU:0, one launch (start us, length us, event | category | flops | bytes accessed | tf_op | source)
XLA Modules:
  0.0 81.8 jit_solution(15690689584253438499)
XLA Ops:
  0.0 0.0 copy-start
  0.0 0.8 copy.30
  0.8 0.1 eq.37
  0.9 0.1 fusion.8
  1.0 0.1 reduce_window_sum.11
  1.1 0.2 select_reduce_fusion
  1.2 0.1 reduce_sum.32
  1.3 0.1 copy.31
  1.4 0.7 multiply_add_fusion
  2.1 0.1 convert_reduce_fusion
  2.2 0.0 copy-done
  2.2 0.4 fusion
  2.6 29.6 %all_to_all.10 = bf16[16,8,3584]{2,1,0:T(8,128)(2,1)S(1)} all-to-all(bf16[16,8,3584]{2,1,0:T(8,128)(2,1)S(1)} %fusion), channel_id=1, replica_groups=mesh['groups'=2,'expert'=16] {'expert'}, dimensions={0} | all-to-all | bytes 1835008 | tf_op jit(solution)/shard_map/all_to_all | solution.py:48
  32.2 1.0 %collective-permute-start = (bf16[16,8,3584]{2,1,0:T(8,128)(2,1)S(1)}, bf16[16,8,3584]{2,1,0:T(8,128)(2,1)S(1)}, u32[]{:S(2)}, u32[]{:S(2)}) collective-permute-start(bf16[16,8,3584]{2,1,0:T(8,128)(2,1)S(1)} %all_to_all.10), channel_id=1, source_target_pairs={{0,1},{1,0},{2,3},{3,2},{4,5},{5,4},{6,7},{7,6},{8,9},{9,8},{10,11... | collective-permute-start | bytes 2752520 | tf_op jit(solution)/shard_map/ppermute | solution.py:14
  33.2 0.0 copy-start.3
  33.2 2.1 %collective-permute-done = bf16[16,8,3584]{2,1,0:T(8,128)(2,1)S(1)} collective-permute-done((bf16[16,8,3584]{2,1,0:T(8,128)(2,1)S(1)}, bf16[16,8,3584]{2,1,0:T(8,128)(2,1)S(1)}, u32[]{:S(2)}, u32[]{:S(2)}) %collective-permute-start) | collective-permute-done | bytes 917536 | tf_op jit(solution)/shard_map/ppermute | solution.py:14
  35.3 0.2 pad_maximum_fusion.1
  35.5 0.0 copy-start.4
  35.5 0.0 copy-done.3
  35.5 1.1 %fusion.5 = f32[256,512]{1,0:T(8,128)S(1)} fusion(bf16[256,3584]{1,0:T(8,128)(2,1)S(1)} %bitcast.36, bf16[1,3584,512]{2,1,0:T(8,128)(2,1)S(1)} %copy-done.3), kind=kOutput, calls=%fused_computation.8 | convolution fusion | flops 939524096 | bytes 6029312 | tf_op jit(solution)/shard_map/dot_general | solution.py:20
  36.6 0.9 %copy-done.4 = bf16[1,3584,512]{2,1,0:T(8,128)(2,1)S(1)} copy-done((bf16[1,3584,512]{2,1,0:T(8,128)(2,1)S(1)}, bf16[1,3584,512]{2,1,0:T(8,128)(2,1)}, u32[]{:S(2)}) %copy-start.4) | copy-done | bytes 3670040
  37.5 0.0 copy-start.1
  37.5 1.1 %multiply_convert_fusion = bf16[256,512]{1,0:T(8,128)(2,1)S(1)} fusion(f32[256,512]{1,0:T(8,128)S(1)} %fusion.5, bf16[256,3584]{1,0:T(8,128)(2,1)S(1)} %bitcast.37, bf16[1,3584,512]{2,1,0:T(8,128)(2,1)S(1)} %copy-done.4), kind=kOutput, calls=%fused_computation.17 | convolution fusion | flops 940310528 | bytes 6291456 | tf_op jit(solution)/shard_map/dot_general | solution.py:21
  38.6 0.9 %copy-done.1 = bf16[1,512,3584]{2,1,0:T(8,128)(2,1)S(1)} copy-done((bf16[1,512,3584]{2,1,0:T(8,128)(2,1)S(1)}, bf16[1,512,3584]{2,1,0:T(8,128)(2,1)}, u32[]{:S(2)}) %copy-start.1) | copy-done | bytes 3670040
  39.5 1.1 %fusion.1 = f32[16,16,3584]{2,1,0:T(8,128)S(1)} fusion(bf16[16,16,512]{2,1,0:T(8,128)(2,1)S(1)} %bitcast.38, bf16[1,512,3584]{2,1,0:T(8,128)(2,1)S(1)} %copy-done.1), kind=kOutput, calls=%fused_computation.4 | convolution fusion | flops 939524096 | bytes 7602176 | tf_op jit(solution)/shard_map/dot_general | solution.py:23
  40.7 0.3 select_bitcast_fusion.1
  41.0 2.1 %copy_bitcast_fusion = f32[16,16,3584]{2,1,0:T(8,128)} fusion(f32[16,1,8,3584]{3,2,0,1:T(8,128)S(1)} %get-tuple-element.6, f32[16,1,8,3584]{3,2,0,1:T(8,128)S(1)} %get-tuple-element.5), kind=kLoop, calls=%fused_computation.10 | loop fusion | flops 917504 | bytes 7340032 | tf_op jit(solution)/shard_map/reshape | solution.py:58
  43.0 0.0 copy-start.2
  43.1 0.4 collective-permute-start.1
  43.4 6.4 %collective-permute-done.1 = f32[16,16,3584]{2,1,0:T(8,128)} collective-permute-done((f32[16,16,3584]{2,1,0:T(8,128)}, f32[16,16,3584]{2,1,0:T(8,128)}, u32[]{:S(2)}, u32[]{:S(2)}) %collective-permute-start.1) | collective-permute-done | bytes 3670048 | tf_op jit(solution)/shard_map/ppermute | solution.py:14
  49.8 3.1 %fusion.7 = bf16[16,16,1792]{2,1,0:T(8,128)(2,1)} fusion(f32[16,16,3584]{2,1,0:T(8,128)} %collective-permute-done.1, s32[]{:T(128)S(6)} %select_n.50, f32[16,16,3584]{2,1,0:T(8,128)} %copy_bitcast_fusion), kind=kLoop, calls=%fused_computation.12 | loop fusion | flops 917504 | bytes 4587524 | tf_op jit(solution)/shard_map/convert_element_type | solution.py:61
  53.0 3.9 %all-to-all-start.1 = ((bf16[16,16,1792]{2,1,0:T(8,128)(2,1)}), bf16[16,16,1792]{2,1,0:T(8,128)(2,1)S(1)}, u32[]{:S(2)}, u32[]{:S(2)}) async-start(bf16[16,16,1792]{2,1,0:T(8,128)(2,1)} %fusion.7), calls=%async_computation.1 | async-start | bytes 1835008 | tf_op jit(solution)/shard_map/all_to_all | solution.py:64
  56.9 0.1 reshape.88
  57.0 0.0 copy-done.2
  57.0 0.1 copy.35
  57.7 19.9 %all-to-all-done.1 = bf16[16,16,1792]{2,1,0:T(8,128)(2,1)S(1)} async-done(((bf16[16,16,1792]{2,1,0:T(8,128)(2,1)}), bf16[16,16,1792]{2,1,0:T(8,128)(2,1)S(1)}, u32[]{:S(2)}, u32[]{:S(2)}) %all-to-all-start.1) | async-done | bytes 917536 | tf_op jit(solution)/shard_map/all_to_all | solution.py:64
  77.7 0.8 copy.34
  78.4 1.5 %gather_fusion = bf16[64,2,1792]{2,1,0:T(2,128)(2,1)S(1)} fusion(bf16[8,2,16,1792]{3,1,2,0:T(2,128)(2,1)S(1)} %copy.34, s32[64]{0:T(128)S(1)} %fusion.15), kind=kCustom, calls=%fused_computation | custom fusion | bytes 918016 | tf_op jit(solution)/shard_map/gather | solution.py:66
  80.0 0.4 reshape.89
  80.4 0.6 multiply_reduce_fusion
  81.0 0.7 select_convert_fusion
  (2 shorter events, 0.0 us)
Async XLA Ops:
  0.0 2.2 %copy-start = (bf16[16,3584]{1,0:T(8,128)(2,1)S(1)}, bf16[16,3584]{1,0:T(8,128)(2,1)}, u32[]{:S(2)}) copy-start(bf16[16,3584]{1,0:T(8,128)(2,1)} %param.7) | copy-start | bytes 344068
  32.2 3.1 %collective-permute-start = (bf16[16,8,3584]{2,1,0:T(8,128)(2,1)S(1)}, bf16[16,8,3584]{2,1,0:T(8,128)(2,1)S(1)}, u32[]{:S(2)}, u32[]{:S(2)}) collective-permute-start(bf16[16,8,3584]{2,1,0:T(8,128)(2,1)S(1)} %all_to_all.10), channel_id=1, source_target_pairs={{0,1},{1,0},{2,3},{3,2},{4,5},{5,4},{6,7},{7,6},{8,9},{9,8},{10,11... | collective-permute-start | bytes 2752520 | tf_op jit(solution)/shard_map/ppermute | solution.py:14
  33.2 2.3 %copy-start.3 = (bf16[1,3584,512]{2,1,0:T(8,128)(2,1)S(1)}, bf16[1,3584,512]{2,1,0:T(8,128)(2,1)}, u32[]{:S(2)}) copy-start(bf16[1,3584,512]{2,1,0:T(8,128)(2,1)} %param.11) | copy-start | bytes 11010052
  35.5 2.0 %copy-start.4 = (bf16[1,3584,512]{2,1,0:T(8,128)(2,1)S(1)}, bf16[1,3584,512]{2,1,0:T(8,128)(2,1)}, u32[]{:S(2)}) copy-start(bf16[1,3584,512]{2,1,0:T(8,128)(2,1)} %param.12) | copy-start | bytes 11010052
  37.5 2.0 %copy-start.1 = (bf16[1,512,3584]{2,1,0:T(8,128)(2,1)S(1)}, bf16[1,512,3584]{2,1,0:T(8,128)(2,1)}, u32[]{:S(2)}) copy-start(bf16[1,512,3584]{2,1,0:T(8,128)(2,1)} %param.13) | copy-start | bytes 11010052
  43.0 13.9 %copy-start.2 = (f32[16,4]{0,1:T(4,128)S(1)}, f32[16,4]{0,1:T(4,128)}, u32[]{:S(2)}) copy-start(f32[16,4]{0,1:T(4,128)} %param.10) | copy-start | bytes 772
  43.1 6.8 %collective-permute-start.1 = (f32[16,16,3584]{2,1,0:T(8,128)}, f32[16,16,3584]{2,1,0:T(8,128)}, u32[]{:S(2)}, u32[]{:S(2)}) collective-permute-start(f32[16,16,3584]{2,1,0:T(8,128)} %copy_bitcast_fusion), channel_id=1, source_target_pairs={{0,1},{1,0},{2,3},{3,2},{4,5},{5,4},{6,7},{7,6},{8,9},{9,8},{10,11... | collective-permute-start | bytes 11010056 | tf_op jit(solution)/shard_map/ppermute | solution.py:14
  53.0 24.7 %all-to-all-start.1 = ((bf16[16,16,1792]{2,1,0:T(8,128)(2,1)}), bf16[16,16,1792]{2,1,0:T(8,128)(2,1)S(1)}, u32[]{:S(2)}, u32[]{:S(2)}) async-start(bf16[16,16,1792]{2,1,0:T(8,128)(2,1)} %fusion.7), calls=%async_computation.1 | async-start | bytes 1835008 | tf_op jit(solution)/shard_map/all_to_all | solution.py:64
where the time goes:
time: 82.8 us; the launch traced here: 81.8 us
  blocking collectives  29.6 us (36%)
  waiting for transfers between devices  28.4 us (34%)
  other arithmetic  8.22 us (10%)
  local copies, waits for them, and re-layouts  5.76 us (7%)
  starting transfers between devices  5.27 us (6%)
  matrix products  3.75 us (5%)
    all_to_all x1, blocking collectives, shards(): lax.all_to_all(outgoing, 'expert', split_axis=0, concat_axis=0, tiled=True)  29.6 us
    all_to_all x1, waiting for transfers between devices, shards(): lax.all_to_all(own_part, 'expert', split_axis=0, concat_axis=0, tiled=True)  19.9 us
    ppermute x2, waiting for transfers between devices, partner_2(): return lax.ppermute(block, axis, route)  8.48 us
    all_to_all x1, starting transfers between devices, shards(): lax.all_to_all(own_part, 'expert', split_axis=0, concat_axis=0, tiled=True)  3.93 us
    convert_element_type x1, other arithmetic, shards(): lax.dynamic_slice_in_dim(summed, parity * half_width, half_width, 2)  3.15 us
    unnamed x12, local copies, waits for them, and re-layouts  2.71 us
    reshape x1, other arithmetic, shards(): partial_value = stacked.reshape(devices, capacity, model_width)  2.07 us
  transfers between devices with their start and end apart: 3, of which 3 were waited for; matrix products, arithmetic and copies ran while one was open for 0% of the time, Pallas kernels for 0%

commit v1 on v0

v1 whole, which is shorter than its diff:
```python
import jax
import jax.numpy as jnp
from jax import lax
from jax.sharding import PartitionSpec as P

LANES = 128


def stage_bits(count):
    top = count.bit_length() - 1
    even = list(range(top - 1, 0, -1))
    odd = even[-1:] + even[:-1]
    return list(zip(even, odd))


def swap(block, bits):
    count = lax.axis_size("expert")
    route = [(i, i ^ (1 << bits[i & 1])) for i in range(count)]
    return lax.ppermute(block, "expert", route)


def gather_rows(rows, count):
    for bits in stage_bits(count):
        rows = jnp.concatenate([rows, swap(rows, bits)], axis=0)
    return rows


def reduce_rows(part, count):
    for bits in stage_bits(count)[::-1]:
        half = part.shape[0] // 2
        got = swap(part[half:].astype(jnp.bfloat16), bits)
        part = part[:half] + got.astype(jnp.float32)
    return part


def routing_columns(live_counts, expert_ids, gate_scores, experts):
    slots = expert_ids.shape[0]
    live = jnp.arange(slots, dtype=jnp.int32)[:, None] < live_counts[0]
    named = expert_ids[:, :, None] == jnp.arange(experts, dtype=jnp.int32)
    score = jnp.sum(jnp.where(named & live[:, :, None], gate_scores[:, :, None], 0.0), axis=1)
    high = lax.reduce_precision(score, 8, 7)
    low = score - high
    pad = jnp.zeros((slots, -2 * experts % LANES), jnp.float32)
    return jnp.concatenate([high, low, pad], axis=1).astype(jnp.bfloat16)


def hidden_rows(rows, width, mine, experts, gate_weight, up_weight):
    inputs, columns = rows[:, :width], rows[:, width:]
    lane = jnp.arange(columns.shape[1], dtype=jnp.int32)
    own = (lane < 2 * experts) & (lane % experts == mine)
    score = jnp.sum(jnp.where(own, columns.astype(jnp.float32), 0.0), axis=1, keepdims=True)
    gate_act = jnp.dot(inputs, gate_weight[0], preferred_element_type=jnp.float32)
    up_act = jnp.dot(inputs, up_weight[0], preferred_element_type=jnp.float32)
    return (jax.nn.silu(gate_act) * up_act).astype(jnp.bfloat16), score


def shards(tokens, live_counts, expert_ids, gate_scores, gate_weight, up_weight, down_weight):
    width = tokens.shape[1]
    count = lax.axis_size("expert")
    experts = count // 2
    mine = lax.shift_right_logical(lax.axis_index("expert"), 1)
    columns = routing_columns(live_counts, expert_ids, gate_scores, experts)
    near = gather_rows(jnp.concatenate([tokens, columns], axis=1), count)
    far = swap(near, (0, 0))
    near_hidden, near_score = hidden_rows(near, width, mine, experts, gate_weight, up_weight)
    far_hidden, far_score = hidden_rows(far, width, mine, experts, gate_weight, up_weight)
    far_part = jnp.dot(far_hidden, down_weight[0], preferred_element_type=jnp.float32) * far_score
    got = swap(far_part.astype(jnp.bfloat16), (0, 0))
    near_part = jnp.dot(near_hidden, down_weight[0], preferred_element_type=jnp.float32) * near_score
    part = near_part + got.astype(jnp.float32)
    return reduce_rows(part, count).astype(jnp.bfloat16)


def solution(mesh):
    in_specs = (
        P(("groups", "expert"), None),
        P(("groups", "expert")),
        P(("groups", "expert"), None),
        P(("groups", "expert"), None),
        P("expert", None, None),
        P("expert", None, None),
        P("expert", None, None),
    )
    out_specs = P(("groups", "expert"), None)
    return jax.shard_map(shards, mesh=mesh, in_specs=in_specs, out_specs=out_specs, check_vma=False)
```

time: 82.8 us -> 69.7 us (0.84); the launches traced: 81.8 us -> 69.5 us
  blocking collectives: 29.6 us -> 0 us
  matrix products: 3.75 us -> 15.3 us
  starting transfers between devices: 5.27 us -> 14.1 us
  waiting for transfers between devices: 28.4 us -> 35.3 us
  other arithmetic: 8.22 us -> 1.78 us
  local copies, waits for them, and re-layouts: 5.76 us -> 2.16 us
    all_to_all x1 -> x0, blocking collectives: 29.6 us -> none  [shards(): lax.all_to_all(outgoing, 'expert', split_axis=0, concat_axis=0, tiled=True)]
    ppermute x2 -> x8, waiting for transfers between devices: 8.48 us -> 35.3 us  [swap(): return lax.ppermute(block, 'expert', route)]
    all_to_all x1 -> x0, waiting for transfers between devices: 19.9 us -> none  [shards(): lax.all_to_all(own_part, 'expert', split_axis=0, concat_axis=0, tiled=True)]
    ppermute x2 -> x8, starting transfers between devices: 1.34 us -> 14.1 us  [swap(): return lax.ppermute(block, 'expert', route)]
    dot_general x4, matrix products: 3.75 us -> 15.3 us  [the longest x1 5.37 us: shards(): jnp.dot(far_hidden, down_weight[0], preferred_element_type=jnp.float32)]
    all_to_all x1 -> x0, starting transfers between devices: 3.93 us -> none  [shards(): lax.all_to_all(own_part, 'expert', split_axis=0, concat_axis=0, tiled=True)]
    convert_element_type x3 -> x1, other arithmetic: 3.95 us -> 0.67 us  [shards(): return reduce_rows(part, count).astype(jnp.bfloat16)]
    reshape x1 -> x0, other arithmetic: 2.07 us -> none  [shards(): partial_value = stacked.reshape(devices, capacity, model_width)]
  transfers between devices with their start and end apart: 3 -> 8, of which waited for: 3 -> 7; matrix products, arithmetic and copies ran while one was open for 0% -> 4% of each run, Pallas kernels for 0% -> 0%
where the time goes in v1:
time: 69.7 us; the launch traced here: 69.5 us
  waiting for transfers between devices  35.3 us (51%)
  matrix products  15.3 us (22%)
  starting transfers between devices  14.1 us (20%)
  local copies, waits for them, and re-layouts  2.16 us (3%)
  other arithmetic  1.78 us (3%)
  between operations  0.78 us (1%)
    ppermute x8, waiting for transfers between devices, swap(): return lax.ppermute(block, 'expert', route)  35.3 us
    ppermute x8, starting transfers between devices, swap(): return lax.ppermute(block, 'expert', route)  14.1 us
    dot_general x1, matrix products, shards(): jnp.dot(far_hidden, down_weight[0], preferred_element_type=jnp.float32)  5.37 us
    dot_general x2, matrix products, hidden_rows(): up_act = jnp.dot(inputs, up_weight[0], preferred_element_type=jnp.float32)  5.35 us
    dot_general x1, matrix products, shards(): jnp.dot(near_hidden, down_weight[0], preferred_element_type=jnp.float32)  4.61 us
  transfers between devices with their start and end apart: 8, of which 7 were waited for; matrix products, arithmetic and copies ran while one was open for 4% of the time, Pallas kernels for 0%

profile of v1, /device:TPU:0, one launch (start us, length us, event | category | flops | bytes accessed | tf_op | source)
XLA Modules:
  0.0 69.5 jit_solution(17607591051968850110)
XLA Ops:
  0.7 0.7 %select_reduce_fusion.2 = f32[16,8]{0,1:T(8,128)S(1)} fusion(f32[16,4]{0,1:T(4,128)} %param.10, s32[16,4]{0,1:T(4,128)} %param.9, pred[16]{0:T(512)(128)(4,1)S(1)} %iota_compare_fusion.1), kind=kLoop, calls=%fused_computation.34 | loop fusion | flops 1920 | bytes 1040 | tf_op jit(solution)/shard_map/reduce_sum | solution.py:40
  1.4 0.1 copy.11
  1.5 0.1 copy.10
  1.6 1.0 %concatenate.17 = bf16[16,3712]{1,0:T(8,128)(2,1)S(1)} concatenate(bf16[16,3584]{1,0:T(8,128)(2,1)} %param.7, bf16[16,8]{1,0:T(8,128)(2,1)S(1)} %copy.10, bf16[16,8]{1,0:T(8,128)(2,1)S(1)} %copy.11, bf16[16,112]{1,0:T(8,128)(2,1)S(1)} %broadcast_in_dim.34), dimensions={1} | concatenate | bytes 237568 | tf_op jit(solution)/shard_map/concatenate | solution.py:63
  2.6 4.1 %collective-permute-start = (bf16[16,3712]{1,0:T(8,128)(2,1)S(1)}, bf16[16,3712]{1,0:T(8,128)(2,1)S(1)}, u32[]{:S(2)}, u32[]{:S(2)}) collective-permute-start(bf16[16,3712]{1,0:T(8,128)(2,1)S(1)} %concatenate.17), channel_id=1, source_target_pairs={{0,8},{1,3},{2,10},{3,1},{4,12},{5,7},{6,14},{7,5},{8,0},{9,11},{1... | collective-permute-start | bytes 356360 | tf_op jit(solution)/shard_map/ppermute | solution.py:19
  6.6 2.8 %collective-permute-done = bf16[16,3712]{1,0:T(8,128)(2,1)S(1)} collective-permute-done((bf16[16,3712]{1,0:T(8,128)(2,1)S(1)}, bf16[16,3712]{1,0:T(8,128)(2,1)S(1)}, u32[]{:S(2)}, u32[]{:S(2)}) %collective-permute-start) | collective-permute-done | bytes 118816 | tf_op jit(solution)/shard_map/ppermute | solution.py:19
  9.5 2.3 %collective-permute-start.1 = (bf16[32,3712]{1,0:T(8,128)(2,1)S(1)}, bf16[32,3712]{1,0:T(8,128)(2,1)S(1)}, u32[]{:S(2)}, u32[]{:S(2)}) collective-permute-start(bf16[32,3712]{1,0:T(8,128)(2,1)S(1)} %pad_maximum_fusion.2), channel_id=1, source_target_pairs={{0,4},{1,9},{2,6},{3,11},{4,0},{5,13},{6,2},{7,15},{8,12},{9,1},{1... | collective-permute-start | bytes 712712 | tf_op jit(solution)/shard_map/ppermute | solution.py:19
  11.8 5.5 %collective-permute-done.1 = bf16[32,3712]{1,0:T(8,128)(2,1)S(1)} collective-permute-done((bf16[32,3712]{1,0:T(8,128)(2,1)S(1)}, bf16[32,3712]{1,0:T(8,128)(2,1)S(1)}, u32[]{:S(2)}, u32[]{:S(2)}) %collective-permute-start.1) | collective-permute-done | bytes 237600 | tf_op jit(solution)/shard_map/ppermute | solution.py:19
  17.3 3.0 %collective-permute-start.2 = (bf16[64,3712]{1,0:T(8,128)(2,1)S(1)}, bf16[64,3712]{1,0:T(8,128)(2,1)S(1)}, u32[]{:S(2)}, u32[]{:S(2)}) collective-permute-start(bf16[64,3712]{1,0:T(8,128)(2,1)S(1)} %pad_maximum_fusion.1), channel_id=1, source_target_pairs={{0,2},{1,5},{2,0},{3,7},{4,6},{5,1},{6,4},{7,3},{8,10},{9,13},{10,... | collective-permute-start | bytes 1425416 | tf_op jit(solution)/shard_map/ppermute | solution.py:19
  20.3 6.6 %collective-permute-done.2 = bf16[64,3712]{1,0:T(8,128)(2,1)S(1)} collective-permute-done((bf16[64,3712]{1,0:T(8,128)(2,1)S(1)}, bf16[64,3712]{1,0:T(8,128)(2,1)S(1)}, u32[]{:S(2)}, u32[]{:S(2)}) %collective-permute-start.2) | collective-permute-done | bytes 475168 | tf_op jit(solution)/shard_map/ppermute | solution.py:19
  26.9 0.1 pad_maximum_fusion
  27.0 0.1 collective-permute-start.3
  27.1 2.5 %collective-permute-done.3 = bf16[128,3712]{1,0:T(8,128)(2,1)S(1)} collective-permute-done((bf16[128,3712]{1,0:T(8,128)(2,1)S(1)}, bf16[128,3712]{1,0:T(8,128)(2,1)S(1)}, u32[]{:S(2)}, u32[]{:S(2)}) %collective-permute-start.3) | collective-permute-done | bytes 950304 | tf_op jit(solution)/shard_map/ppermute | solution.py:19
  29.6 0.1 select_reduce_fusion.1
  29.7 2.7 %fusion.3 = f32[128,512]{1,0:T(8,128)S(1)} fusion(bf16[1,3584,512]{2,1,0:T(8,128)(2,1)} %param.12, bf16[128,3712]{1,0:T(8,128)(2,1)S(1)} %collective-permute-done.3), kind=kOutput, calls=%fused_computation.4 | convolution fusion | flops 469762048 | bytes 4849664 | tf_op jit(solution)/shard_map/dot_general | solution.py:53
  32.4 5.4 %multiply_convert_fusion = bf16[128,3584]{1,0:T(8,128)(2,1)} fusion(f32[128]{0:T(128)S(1)} %get-tuple-element.6, bf16[1,512,3584]{2,1,0:T(8,128)(2,1)} %param.13, f32[128,512]{1,0:T(8,128)S(1)} %fusion.3, bf16[1,3584,512]{2,1,0:T(8,128)(2,1)} %param.11, bf16[128,3712]{1,0:T(8,128)(2,1)S(1)} %collective-permute-done.3), kind=kOutput, calls=%fused_computation.13 | convolution fusion | flops 940834816 | bytes 9437696 | tf_op jit(solution)/shard_map/dot_general | solution.py:67
  37.7 0.1 collective-permute-start.4
  37.9 2.7 %fusion.5 = f32[128,512]{1,0:T(8,128)S(1)} fusion(bf16[1,3584,512]{2,1,0:T(8,128)(2,1)} %param.12, bf16[128,3712]{1,0:T(8,128)(2,1)S(1)} %pad_maximum_fusion), kind=kOutput, calls=%fused_computation.6 | convolution fusion | flops 469762048 | bytes 4849664 | tf_op jit(solution)/shard_map/dot_general | solution.py:53
  40.6 0.0 collective-permute-done.4
  40.6 0.0 copy-start
  40.6 0.9 %copy-done = bf16[128,3584]{1,0:T(8,128)(2,1)} copy-done((bf16[128,3584]{1,0:T(8,128)(2,1)}, bf16[128,3584]{1,0:T(8,128)(2,1)S(1)}, u32[]{:S(2)}) %copy-start) | copy-done | bytes 917528
  41.5 4.6 %convert_add_fusion = f32[128,3584]{1,0:T(8,128)S(1)} fusion(bf16[128,3584]{1,0:T(8,128)(2,1)} %copy-done, f32[128]{0:T(128)S(1)} %get-tuple-element.5, bf16[1,512,3584]{2,1,0:T(8,128)(2,1)} %param.13, f32[128,512]{1,0:T(8,128)S(1)} %fusion.5, bf16[1,3584,512]{2,1,0:T(8,128)(2,1)} %param.11, bf16[128,3712]{1,0:T(8,128)(2,1)S(1)} %pad_maximum_fusion), kind=kOutput, calls=%fused_computation.12 | convolution fusion | flops 941293568 | bytes 11272704 | tf_op jit(solution)/shard_map/dot_general | solution.py:69
  46.2 2.1 %collective-permute-start.5 = (bf16[64,3584]{1,0:T(8,128)(2,1)S(1)}, bf16[64,3584]{1,0:T(8,128)(2,1)S(1)}, u32[]{:S(2)}, u32[]{:S(2)}) collective-permute-start(bf16[64,3584]{1,0:T(8,128)(2,1)S(1)} %slice.79), channel_id=1, source_target_pairs={{0,2},{1,5},{2,0},{3,7},{4,6},{5,1},{6,4},{7,3},{8,10},{9,13},{10,... | collective-permute-start | bytes 1376264 | tf_op jit(solution)/shard_map/ppermute | solution.py:19
  48.3 6.5 %collective-permute-done.5 = bf16[64,3584]{1,0:T(8,128)(2,1)S(1)} collective-permute-done((bf16[64,3584]{1,0:T(8,128)(2,1)S(1)}, bf16[64,3584]{1,0:T(8,128)(2,1)S(1)}, u32[]{:S(2)}, u32[]{:S(2)}) %collective-permute-start.5) | collective-permute-done | bytes 458784 | tf_op jit(solution)/shard_map/ppermute | solution.py:19
  54.7 0.1 slice_add_fusion
  54.8 0.1 collective-permute-start.6
  54.9 8.1 %collective-permute-done.6 = bf16[32,3584]{1,0:T(8,128)(2,1)S(1)} collective-permute-done((bf16[32,3584]{1,0:T(8,128)(2,1)S(1)}, bf16[32,3584]{1,0:T(8,128)(2,1)S(1)}, u32[]{:S(2)}, u32[]{:S(2)}) %collective-permute-start.6) | collective-permute-done | bytes 229408 | tf_op jit(solution)/shard_map/ppermute | solution.py:19
  63.0 0.1 slice_add_fusion.1
  63.1 2.4 %collective-permute-start.7 = (bf16[16,3584]{1,0:T(8,128)(2,1)S(1)}, bf16[16,3584]{1,0:T(8,128)(2,1)S(1)}, u32[]{:S(2)}, u32[]{:S(2)}) collective-permute-start(bf16[16,3584]{1,0:T(8,128)(2,1)S(1)} %slice.81), channel_id=1, source_target_pairs={{0,8},{1,3},{2,10},{3,1},{4,12},{5,7},{6,14},{7,5},{8,0},{9,11},{1... | collective-permute-start | bytes 344072 | tf_op jit(solution)/shard_map/ppermute | solution.py:19
  65.5 3.4 %collective-permute-done.7 = bf16[16,3584]{1,0:T(8,128)(2,1)S(1)} collective-permute-done((bf16[16,3584]{1,0:T(8,128)(2,1)S(1)}, bf16[16,3584]{1,0:T(8,128)(2,1)S(1)}, u32[]{:S(2)}, u32[]{:S(2)}) %collective-permute-start.7) | collective-permute-done | bytes 114720 | tf_op jit(solution)/shard_map/ppermute | solution.py:19
  68.8 0.7 fusion.17
  (9 shorter events, 0.2 us)
Async XLA Ops:
  2.6 6.9 %collective-permute-start = (bf16[16,3712]{1,0:T(8,128)(2,1)S(1)}, bf16[16,3712]{1,0:T(8,128)(2,1)S(1)}, u32[]{:S(2)}, u32[]{:S(2)}) collective-permute-start(bf16[16,3712]{1,0:T(8,128)(2,1)S(1)} %concatenate.17), channel_id=1, source_target_pairs={{0,8},{1,3},{2,10},{3,1},{4,12},{5,7},{6,14},{7,5},{8,0},{9,11},{1... | collective-permute-start | bytes 356360 | tf_op jit(solution)/shard_map/ppermute | solution.py:19
  9.5 7.8 %collective-permute-start.1 = (bf16[32,3712]{1,0:T(8,128)(2,1)S(1)}, bf16[32,3712]{1,0:T(8,128)(2,1)S(1)}, u32[]{:S(2)}, u32[]{:S(2)}) collective-permute-start(bf16[32,3712]{1,0:T(8,128)(2,1)S(1)} %pad_maximum_fusion.2), channel_id=1, source_target_pairs={{0,4},{1,9},{2,6},{3,11},{4,0},{5,13},{6,2},{7,15},{8,12},{9,1},{1... | collective-permute-start | bytes 712712 | tf_op jit(solution)/shard_map/ppermute | solution.py:19
  17.3 9.6 %collective-permute-start.2 = (bf16[64,3712]{1,0:T(8,128)(2,1)S(1)}, bf16[64,3712]{1,0:T(8,128)(2,1)S(1)}, u32[]{:S(2)}, u32[]{:S(2)}) collective-permute-start(bf16[64,3712]{1,0:T(8,128)(2,1)S(1)} %pad_maximum_fusion.1), channel_id=1, source_target_pairs={{0,2},{1,5},{2,0},{3,7},{4,6},{5,1},{6,4},{7,3},{8,10},{9,13},{10,... | collective-permute-start | bytes 1425416 | tf_op jit(solution)/shard_map/ppermute | solution.py:19
  27.0 2.6 %collective-permute-start.3 = (bf16[128,3712]{1,0:T(8,128)(2,1)S(1)}, bf16[128,3712]{1,0:T(8,128)(2,1)S(1)}, u32[]{:S(2)}, u32[]{:S(2)}) collective-permute-start(bf16[128,3712]{1,0:T(8,128)(2,1)S(1)} %pad_maximum_fusion), channel_id=1, source_target_pairs={{0,1},{1,0},{2,3},{3,2},{4,5},{5,4},{6,7},{7,6},{8,9},{9,8},{10,11... | collective-permute-start | bytes 2850824 | tf_op jit(solution)/shard_map/ppermute | solution.py:19
  37.7 2.8 %collective-permute-start.4 = (bf16[128,3584]{1,0:T(8,128)(2,1)}, bf16[128,3584]{1,0:T(8,128)(2,1)S(1)}, u32[]{:S(2)}, u32[]{:S(2)}) collective-permute-start(bf16[128,3584]{1,0:T(8,128)(2,1)} %multiply_convert_fusion), channel_id=1, source_target_pairs={{0,1},{1,0},{2,3},{3,2},{4,5},{5,4},{6,7},{7,6},{8,9},{9,8},{10,11... | collective-permute-start | bytes 2752520 | tf_op jit(solution)/shard_map/ppermute | solution.py:19
  40.6 0.9 %copy-start = (bf16[128,3584]{1,0:T(8,128)(2,1)}, bf16[128,3584]{1,0:T(8,128)(2,1)S(1)}, u32[]{:S(2)}) copy-start(bf16[128,3584]{1,0:T(8,128)(2,1)S(1)} %collective-permute-done.4) | copy-start | bytes 2752516
  46.2 8.5 %collective-permute-start.5 = (bf16[64,3584]{1,0:T(8,128)(2,1)S(1)}, bf16[64,3584]{1,0:T(8,128)(2,1)S(1)}, u32[]{:S(2)}, u32[]{:S(2)}) collective-permute-start(bf16[64,3584]{1,0:T(8,128)(2,1)S(1)} %slice.79), channel_id=1, source_target_pairs={{0,2},{1,5},{2,0},{3,7},{4,6},{5,1},{6,4},{7,3},{8,10},{9,13},{10,... | collective-permute-start | bytes 1376264 | tf_op jit(solution)/shard_map/ppermute | solution.py:19
  54.8 8.2 %collective-permute-start.6 = (bf16[32,3584]{1,0:T(8,128)(2,1)S(1)}, bf16[32,3584]{1,0:T(8,128)(2,1)S(1)}, u32[]{:S(2)}, u32[]{:S(2)}) collective-permute-start(bf16[32,3584]{1,0:T(8,128)(2,1)S(1)} %slice.80), channel_id=1, source_target_pairs={{0,4},{1,9},{2,6},{3,11},{4,0},{5,13},{6,2},{7,15},{8,12},{9,1},{1... | collective-permute-start | bytes 688136 | tf_op jit(solution)/shard_map/ppermute | solution.py:19
  63.1 5.8 %collective-permute-start.7 = (bf16[16,3584]{1,0:T(8,128)(2,1)S(1)}, bf16[16,3584]{1,0:T(8,128)(2,1)S(1)}, u32[]{:S(2)}, u32[]{:S(2)}) collective-permute-start(bf16[16,3584]{1,0:T(8,128)(2,1)S(1)} %slice.81), channel_id=1, source_target_pairs={{0,8},{1,3},{2,10},{3,1},{4,12},{5,7},{6,14},{7,5},{8,0},{9,11},{1... | collective-permute-start | bytes 344072 | tf_op jit(solution)/shard_map/ppermute | solution.py:19

commit v2 on v1

--- a/solution.py
+++ b/solution.py
@@ -1,6 +1,8 @@
 import jax
 import jax.numpy as jnp
 from jax import lax
+from jax.experimental import pallas as pl
+from jax.experimental.pallas import tpu as pltpu
 from jax.sharding import PartitionSpec as P
 
 LANES = 128
@@ -44,14 +46,68 @@
     return jnp.concatenate([high, low, pad], axis=1).astype(jnp.bfloat16)
 
 
-def hidden_rows(rows, width, mine, experts, gate_weight, up_weight):
-    inputs, columns = rows[:, :width], rows[:, width:]
-    lane = jnp.arange(columns.shape[1], dtype=jnp.int32)
-    own = (lane < 2 * experts) & (lane % experts == mine)
-    score = jnp.sum(jnp.where(own, columns.astype(jnp.float32), 0.0), axis=1, keepdims=True)
-    gate_act = jnp.dot(inputs, gate_weight[0], preferred_element_type=jnp.float32)
-    up_act = jnp.dot(inputs, up_weight[0], preferred_element_type=jnp.float32)
-    return (jax.nn.silu(gate_act) * up_act).astype(jnp.bfloat16), score
+def expert_body(rows, score, gate_a, up_a, down_a, gate_b, up_b, down_b, out):
+    step, steps = pl.program_id(1), pl.num_programs(1)
+    inputs = rows[:, : out.shape[1]]
+
+    def add_units(gate, up, down):
+        gate_act = jnp.dot(inputs, gate[0], preferred_element_type=jnp.float32)
+        up_act = jnp.dot(inputs, up[0], preferred_element_type=jnp.float32)
+        hidden = (gate_act / (1.0 + jnp.exp(-gate_act)) * up_act).astype(jnp.bfloat16)
+        return jnp.dot(hidden, down[0], preferred_element_type=jnp.float32)
+
+    @pl.when(step == 0)
+    def _():
+        out[...] = add_units(gate_a, up_a, down_a)
+
+    @pl.when((step > 0) & (step < steps // 2))
+    def _():
+        out[...] += add_units(gate_a, up_a, down_a)
+
+    @pl.when((step >= steps // 2) & (step < steps - 1))
+    def _():
+        out[...] += add_units(gate_b, up_b, down_b)
+
+    @pl.when(step == steps - 1)
+    def _():
+        out[...] = (out[...] + add_units(gate_b, up_b, down_b)) * score[...]
+
+
+def expert_rows(rows, score, own, other):
+    count, units, width = rows.shape[0], own[2].shape[1], own[2].shape[2]
+    tile = min(count, 256)
+    block = min(units, 256)
+    half = units // block
+
+    def first(j):
+        return jnp.minimum(j, half - 1)
+
+    def second(j):
+        return jnp.maximum(j - half, 0)
+
+    def specs(at):
+        side = pl.BlockSpec((1, width, block), lambda i, j: (0, 0, at(j)))
+        return [side, side, pl.BlockSpec((1, block, width), lambda i, j: (0, at(j), 0))]
+
+    return pl.pallas_call(
+        expert_body,
+        grid=(count // tile, 2 * half),
+        in_specs=[
+            pl.BlockSpec((tile, rows.shape[1]), lambda i, j: (i, 0)),
+            pl.BlockSpec((tile, 1), lambda i, j: (i, 0)),
+        ]
+        + specs(first)
+        + specs(second),
+        out_specs=pl.BlockSpec((tile, width), lambda i, j: (i, 0)),
+        out_shape=jax.ShapeDtypeStruct((count, width), jnp.float32),
+        compiler_params=pltpu.CompilerParams(
+            dimension_semantics=("arbitrary", "arbitrary"), vmem_limit_bytes=50 * 2**20
+        ),
+        cost_estimate=pl.CostEstimate(
+            flops=12 * count * units * width, bytes_accessed=12 * units * width, transcendentals=0
+        ),
+        name="experts",
+    )(rows, score, *own, *other)
 
 
 def shards(tokens, live_counts, expert_ids, gate_scores, gate_weight, up_weight, down_weight):
@@ -59,15 +115,15 @@
     count = lax.axis_size("expert")
     experts = count // 2
     mine = lax.shift_right_logical(lax.axis_index("expert"), 1)
+    own = (gate_weight, up_weight, down_weight)
+    other = [swap(weight, (0, 0)) for weight in own]
     columns = routing_columns(live_counts, expert_ids, gate_scores, experts)
-    near = gather_rows(jnp.concatenate([tokens, columns], axis=1), count)
-    far = swap(near, (0, 0))
-    near_hidden, near_score = hidden_rows(near, width, mine, experts, gate_weight, up_weight)
-    far_hidden, far_score = hidden_rows(far, width, mine, experts, gate_weight, up_weight)
-    far_part = jnp.dot(far_hidden, down_weight[0], preferred_element_type=jnp.float32) * far_score
-    got = swap(far_part.astype(jnp.bfloat16), (0, 0))
-    near_part = jnp.dot(near_hidden, down_weight[0], preferred_element_type=jnp.float32) * near_score
-    part = near_part + got.astype(jnp.float32)
+    rows = gather_rows(jnp.concatenate([tokens, columns], axis=1), count)
+    columns = rows[:, width:]
+    lane = jnp.arange(columns.shape[1], dtype=jnp.int32)
+    named = (lane < 2 * experts) & (lane % experts == mine)
+    score = jnp.sum(jnp.where(named, columns.astype(jnp.float32), 0.0), axis=1, keepdims=True)
+    part = expert_rows(rows, score, own, other)
     return reduce_rows(part, count).astype(jnp.bfloat16)
 
 

time: 69.7 us -> 62.6 us (0.90)
  matrix products: 15.3 us -> 0 us
  Pallas kernels: 0 us -> 10.7 us
  waiting for transfers between devices: 35.3 us -> 33.7 us
  local copies, waits for them, and re-layouts: 2.16 us -> 1.34 us
    dot_general x4 -> x0, matrix products: 15.3 us -> none  [the longest x1 5.37 us: shards(): jnp.dot(far_hidden, down_weight[0], preferred_element_type=jnp.float32)]
    pallas_call x0 -> x1, Pallas kernels: none -> 10.7 us  [expert_rows(): pl.pallas_call(expert_body, grid=(count // tile, 2 * half), in_specs=[pl....]
    ppermute x8 -> x9, waiting for transfers between devices: 35.3 us -> 33.7 us  [swap(): return lax.ppermute(block, 'expert', route)]
    unnamed x2 -> x0, local copies, waits for them, and re-layouts: 0.91 us -> none
    ppermute x8 -> x9, starting transfers between devices: 14.1 us -> 14.2 us  [swap(): return lax.ppermute(block, 'expert', route)]
  transfers between devices with their start and end apart: 8 -> 9, of which waited for: 7 -> 6; matrix products, arithmetic and copies ran while one was open for 4% -> 4% of each run, Pallas kernels for 0% -> 0%
where the time goes in v2:
time: 62.6 us; the launch traced here: 62.4 us
  waiting for transfers between devices  33.7 us (54%)
  starting transfers between devices  14.2 us (23%)
  Pallas kernels  10.7 us (17%)
  other arithmetic  1.78 us (3%)
  local copies, waits for them, and re-layouts  1.34 us (2%)
  between operations  0.76 us (1%)
    ppermute x9, waiting for transfers between devices, swap(): return lax.ppermute(block, 'expert', route)  33.7 us
    ppermute x9, starting transfers between devices, swap(): return lax.ppermute(block, 'expert', route)  14.2 us
    pallas_call x1, Pallas kernels, expert_rows(): pl.pallas_call(expert_body, grid=(count // tile, 2 * half), in_specs=[pl....  10.7 us
  transfers between devices with their start and end apart: 9, of which 6 were waited for; matrix products, arithmetic and copies ran while one was open for 4% of the time, Pallas kernels for 0%

profile of v2, /device:TPU:0, one launch (start us, length us, event | category | flops | bytes accessed | tf_op | source)
XLA Modules:
  0.0 62.4 jit_solution(4727332105774463345)
XLA Ops:
  0.0 0.5 collective-permute-start.3
  0.5 0.0 collective-permute-start.4
  0.5 0.5 collective-permute-start.5
  1.7 0.7 %select_reduce_fusion.1 = f32[16,8]{0,1:T(8,128)S(1)} fusion(f32[16,4]{0,1:T(4,128)} %param.10, s32[16,4]{0,1:T(4,128)} %param.9, pred[16]{0:T(512)(128)(4,1)S(1)} %iota_compare_fusion.1), kind=kLoop, calls=%fused_computation.11 | loop fusion | flops 1920 | bytes 1040 | tf_op jit(solution)/shard_map/reduce_sum | solution.py:42
  2.4 0.1 copy.15
  2.5 0.1 copy.14
  2.5 1.0 %concatenate.17 = bf16[16,3712]{1,0:T(8,128)(2,1)S(1)} concatenate(bf16[16,3584]{1,0:T(8,128)(2,1)} %param.7, bf16[16,8]{1,0:T(8,128)(2,1)S(1)} %get-tuple-element.6, bf16[16,8]{1,0:T(8,128)(2,1)S(1)} %get-tuple-element.5, bf16[16,112]{1,0:T(8,128)(2,1)S(1)} %broadcast_in_dim.33), dimensions={1} | concatenate | bytes 237568 | tf_op jit(solution)/shard_map/concatenate | solution.py:121
  3.5 3.6 %collective-permute-start = (bf16[16,3712]{1,0:T(8,128)(2,1)S(1)}, bf16[16,3712]{1,0:T(8,128)(2,1)S(1)}, u32[]{:S(2)}, u32[]{:S(2)}) collective-permute-start(bf16[16,3712]{1,0:T(8,128)(2,1)S(1)} %concatenate.17), channel_id=1, source_target_pairs={{0,8},{1,3},{2,10},{3,1},{4,12},{5,7},{6,14},{7,5},{8,0},{9,11},{1... | collective-permute-start | bytes 356360 | tf_op jit(solution)/shard_map/ppermute | solution.py:21
  7.1 2.8 %collective-permute-done = bf16[16,3712]{1,0:T(8,128)(2,1)S(1)} collective-permute-done((bf16[16,3712]{1,0:T(8,128)(2,1)S(1)}, bf16[16,3712]{1,0:T(8,128)(2,1)S(1)}, u32[]{:S(2)}, u32[]{:S(2)}) %collective-permute-start) | collective-permute-done | bytes 118816 | tf_op jit(solution)/shard_map/ppermute | solution.py:21
  10.0 2.3 %collective-permute-start.1 = (bf16[32,3712]{1,0:T(8,128)(2,1)S(1)}, bf16[32,3712]{1,0:T(8,128)(2,1)S(1)}, u32[]{:S(2)}, u32[]{:S(2)}) collective-permute-start(bf16[32,3712]{1,0:T(8,128)(2,1)S(1)} %pad_maximum_fusion.2), channel_id=1, source_target_pairs={{0,4},{1,9},{2,6},{3,11},{4,0},{5,13},{6,2},{7,15},{8,12},{9,1},{1... | collective-permute-start | bytes 712712 | tf_op jit(solution)/shard_map/ppermute | solution.py:21
  12.3 5.5 %collective-permute-done.1 = bf16[32,3712]{1,0:T(8,128)(2,1)S(1)} collective-permute-done((bf16[32,3712]{1,0:T(8,128)(2,1)S(1)}, bf16[32,3712]{1,0:T(8,128)(2,1)S(1)}, u32[]{:S(2)}, u32[]{:S(2)}) %collective-permute-start.1) | collective-permute-done | bytes 237600 | tf_op jit(solution)/shard_map/ppermute | solution.py:21
  17.8 3.0 %collective-permute-start.2 = (bf16[64,3712]{1,0:T(8,128)(2,1)S(1)}, bf16[64,3712]{1,0:T(8,128)(2,1)S(1)}, u32[]{:S(2)}, u32[]{:S(2)}) collective-permute-start(bf16[64,3712]{1,0:T(8,128)(2,1)S(1)} %pad_maximum_fusion.1), channel_id=1, source_target_pairs={{0,2},{1,5},{2,0},{3,7},{4,6},{5,1},{6,4},{7,3},{8,10},{9,13},{10,... | collective-permute-start | bytes 1425416 | tf_op jit(solution)/shard_map/ppermute | solution.py:21
  20.8 6.6 %collective-permute-done.2 = bf16[64,3712]{1,0:T(8,128)(2,1)S(1)} collective-permute-done((bf16[64,3712]{1,0:T(8,128)(2,1)S(1)}, bf16[64,3712]{1,0:T(8,128)(2,1)S(1)}, u32[]{:S(2)}, u32[]{:S(2)}) %collective-permute-start.2) | collective-permute-done | bytes 475168 | tf_op jit(solution)/shard_map/ppermute | solution.py:21
  27.4 0.1 pad_maximum_fusion.rows
  27.5 0.1 select_reduce_fusion
  27.6 0.1 copy.17.score
  27.7 0.0 collective-permute-done.3.gate_b
  27.7 0.0 collective-permute-done.4.up_b
  27.7 0.0 collective-permute-done.5.down_b
  27.7 10.7 %experts.1 = f32[128,3584]{1,0:T(8,128)S(1)} custom-call(bf16[128,3712]{1,0:T(8,128)(2,1)S(1)} %pad_maximum_fusion.rows, f32[128,1]{1,0:T(8,128)S(1)} %copy.17.score, bf16[1,3584,512]{2,1,0:T(8,128)(2,1)} %gate_a.1, bf16[1,3584,512]{2,1,0:T(8,128)(2,1)} %up_a.1, bf16[1,512,3584]{2,1,0:T(8,128)(2,1)} %down_a.1, ...), custom_call_target="tpu_custom_call" | custom-call | flops 2818572288 | bytes 22020096 | tf_op jit(solution)/shard_map/experts/pallas_call | solution.py:92
  38.5 2.1 %collective-permute-start.6 = (bf16[64,3584]{1,0:T(8,128)(2,1)S(1)}, bf16[64,3584]{1,0:T(8,128)(2,1)S(1)}, u32[]{:S(2)}, u32[]{:S(2)}) collective-permute-start(bf16[64,3584]{1,0:T(8,128)(2,1)S(1)} %slice.47), channel_id=1, source_target_pairs={{0,2},{1,5},{2,0},{3,7},{4,6},{5,1},{6,4},{7,3},{8,10},{9,13},{10,... | collective-permute-start | bytes 1376264 | tf_op jit(solution)/shard_map/ppermute | solution.py:21
  40.5 6.5 %collective-permute-done.6 = bf16[64,3584]{1,0:T(8,128)(2,1)S(1)} collective-permute-done((bf16[64,3584]{1,0:T(8,128)(2,1)S(1)}, bf16[64,3584]{1,0:T(8,128)(2,1)S(1)}, u32[]{:S(2)}, u32[]{:S(2)}) %collective-permute-start.6) | collective-permute-done | bytes 458784 | tf_op jit(solution)/shard_map/ppermute | solution.py:21
  47.0 0.1 slice_add_fusion
  47.1 0.5 collective-permute-start.7
  47.7 7.0 %collective-permute-done.7 = bf16[32,3584]{1,0:T(8,128)(2,1)S(1)} collective-permute-done((bf16[32,3584]{1,0:T(8,128)(2,1)S(1)}, bf16[32,3584]{1,0:T(8,128)(2,1)S(1)}, u32[]{:S(2)}, u32[]{:S(2)}) %collective-permute-start.7) | collective-permute-done | bytes 229408 | tf_op jit(solution)/shard_map/ppermute | solution.py:21
  54.7 0.1 slice_add_fusion.1
  54.8 1.7 %collective-permute-start.8 = (bf16[16,3584]{1,0:T(8,128)(2,1)S(1)}, bf16[16,3584]{1,0:T(8,128)(2,1)S(1)}, u32[]{:S(2)}, u32[]{:S(2)}) collective-permute-start(bf16[16,3584]{1,0:T(8,128)(2,1)S(1)} %slice.49), channel_id=1, source_target_pairs={{0,8},{1,3},{2,10},{3,1},{4,12},{5,7},{6,14},{7,5},{8,0},{9,11},{1... | collective-permute-start | bytes 344072 | tf_op jit(solution)/shard_map/ppermute | solution.py:21
  56.5 5.3 %collective-permute-done.8 = bf16[16,3584]{1,0:T(8,128)(2,1)S(1)} collective-permute-done((bf16[16,3584]{1,0:T(8,128)(2,1)S(1)}, bf16[16,3584]{1,0:T(8,128)(2,1)S(1)}, u32[]{:S(2)}, u32[]{:S(2)}) %collective-permute-start.8) | collective-permute-done | bytes 114720 | tf_op jit(solution)/shard_map/ppermute | solution.py:21
  61.7 0.7 %fusion = bf16[16,3584]{1,0:T(8,128)(2,1)} fusion(f32[32,3584]{1,0:T(8,128)S(1)} %slice_add_fusion.1, bf16[16,3584]{1,0:T(8,128)(2,1)S(1)} %collective-permute-done.8), kind=kLoop, calls=%fused_computation.9 | loop fusion | flops 172032 | bytes 458752 | tf_op jit(solution)/shard_map/convert_element_type | solution.py:127
  (10 shorter events, 0.2 us)
Async XLA Ops:
  0.0 27.7 %collective-permute-start.3 = (bf16[1,3584,512]{2,1,0:T(8,128)(2,1)}, bf16[1,3584,512]{2,1,0:T(8,128)(2,1)}, u32[]{:S(2)}, u32[]{:S(2)}) collective-permute-start(bf16[1,3584,512]{2,1,0:T(8,128)(2,1)} %gate_a.1), channel_id=1, source_target_pairs={{0,1},{1,0},{2,3},{3,2},{4,5},{5,4},{6,7},{7,6},{8,9},{9,8},{10,11... | collective-permute-start | bytes 11010056 | tf_op jit(solution)/shard_map/ppermute | solution.py:21
  0.5 27.2 %collective-permute-start.4 = (bf16[1,3584,512]{2,1,0:T(8,128)(2,1)}, bf16[1,3584,512]{2,1,0:T(8,128)(2,1)}, u32[]{:S(2)}, u32[]{:S(2)}) collective-permute-start(bf16[1,3584,512]{2,1,0:T(8,128)(2,1)} %up_a.1), channel_id=1, source_target_pairs={{0,1},{1,0},{2,3},{3,2},{4,5},{5,4},{6,7},{7,6},{8,9},{9,8},{10,11... | collective-permute-start | bytes 11010056 | tf_op jit(solution)/shard_map/ppermute | solution.py:21
  0.5 27.2 %collective-permute-start.5 = (bf16[1,512,3584]{2,1,0:T(8,128)(2,1)}, bf16[1,512,3584]{2,1,0:T(8,128)(2,1)}, u32[]{:S(2)}, u32[]{:S(2)}) collective-permute-start(bf16[1,512,3584]{2,1,0:T(8,128)(2,1)} %down_a.1), channel_id=1, source_target_pairs={{0,1},{1,0},{2,3},{3,2},{4,5},{5,4},{6,7},{7,6},{8,9},{9,8},{10,11... | collective-permute-start | bytes 11010056 | tf_op jit(solution)/shard_map/ppermute | solution.py:21
  3.5 6.4 %collective-permute-start = (bf16[16,3712]{1,0:T(8,128)(2,1)S(1)}, bf16[16,3712]{1,0:T(8,128)(2,1)S(1)}, u32[]{:S(2)}, u32[]{:S(2)}) collective-permute-start(bf16[16,3712]{1,0:T(8,128)(2,1)S(1)} %concatenate.17), channel_id=1, source_target_pairs={{0,8},{1,3},{2,10},{3,1},{4,12},{5,7},{6,14},{7,5},{8,0},{9,11},{1... | collective-permute-start | bytes 356360 | tf_op jit(solution)/shard_map/ppermute | solution.py:21
  10.0 7.8 %collective-permute-start.1 = (bf16[32,3712]{1,0:T(8,128)(2,1)S(1)}, bf16[32,3712]{1,0:T(8,128)(2,1)S(1)}, u32[]{:S(2)}, u32[]{:S(2)}) collective-permute-start(bf16[32,3712]{1,0:T(8,128)(2,1)S(1)} %pad_maximum_fusion.2), channel_id=1, source_target_pairs={{0,4},{1,9},{2,6},{3,11},{4,0},{5,13},{6,2},{7,15},{8,12},{9,1},{1... | collective-permute-start | bytes 712712 | tf_op jit(solution)/shard_map/ppermute | solution.py:21
  17.8 9.6 %collective-permute-start.2 = (bf16[64,3712]{1,0:T(8,128)(2,1)S(1)}, bf16[64,3712]{1,0:T(8,128)(2,1)S(1)}, u32[]{:S(2)}, u32[]{:S(2)}) collective-permute-start(bf16[64,3712]{1,0:T(8,128)(2,1)S(1)} %pad_maximum_fusion.1), channel_id=1, source_target_pairs={{0,2},{1,5},{2,0},{3,7},{4,6},{5,1},{6,4},{7,3},{8,10},{9,13},{10,... | collective-permute-start | bytes 1425416 | tf_op jit(solution)/shard_map/ppermute | solution.py:21
  38.5 8.5 %collective-permute-start.6 = (bf16[64,3584]{1,0:T(8,128)(2,1)S(1)}, bf16[64,3584]{1,0:T(8,128)(2,1)S(1)}, u32[]{:S(2)}, u32[]{:S(2)}) collective-permute-start(bf16[64,3584]{1,0:T(8,128)(2,1)S(1)} %slice.47), channel_id=1, source_target_pairs={{0,2},{1,5},{2,0},{3,7},{4,6},{5,1},{6,4},{7,3},{8,10},{9,13},{10,... | collective-permute-start | bytes 1376264 | tf_op jit(solution)/shard_map/ppermute | solution.py:21
  47.1 7.5 %collective-permute-start.7 = (bf16[32,3584]{1,0:T(8,128)(2,1)S(1)}, bf16[32,3584]{1,0:T(8,128)(2,1)S(1)}, u32[]{:S(2)}, u32[]{:S(2)}) collective-permute-start(bf16[32,3584]{1,0:T(8,128)(2,1)S(1)} %slice.48), channel_id=1, source_target_pairs={{0,4},{1,9},{2,6},{3,11},{4,0},{5,13},{6,2},{7,15},{8,12},{9,1},{1... | collective-permute-start | bytes 688136 | tf_op jit(solution)/shard_map/ppermute | solution.py:21
  54.8 7.0 %collective-permute-start.8 = (bf16[16,3584]{1,0:T(8,128)(2,1)S(1)}, bf16[16,3584]{1,0:T(8,128)(2,1)S(1)}, u32[]{:S(2)}, u32[]{:S(2)}) collective-permute-start(bf16[16,3584]{1,0:T(8,128)(2,1)S(1)} %slice.49), channel_id=1, source_target_pairs={{0,8},{1,3},{2,10},{3,1},{4,12},{5,7},{6,14},{7,5},{8,0},{9,11},{1... | collective-permute-start | bytes 344072 | tf_op jit(solution)/shard_map/ppermute | solution.py:21

commit v3 on v1

v3 whole, which is shorter than its diff:
```python
import jax
import jax.numpy as jnp
from jax import lax
from jax.experimental import pallas as pl
from jax.experimental.pallas import tpu as pltpu
from jax.sharding import PartitionSpec as P

LANES = 128


def stage_bits(count):
    top = count.bit_length() - 1
    even = list(range(top - 1, 0, -1))
    odd = even[-1:] + even[:-1]
    return list(zip(even, odd))


def swap(block, bits):
    count = lax.axis_size("expert")
    route = [(i, i ^ (1 << bits[i & 1])) for i in range(count)]
    return lax.ppermute(block, "expert", route)


def gather_rows(rows, stages):
    for bits in stages:
        rows = jnp.concatenate([rows, swap(rows, bits)], axis=0)
    return rows


def reduce_rows(part, count):
    for bits in stage_bits(count)[::-1]:
        half = part.shape[0] // 2
        got = swap(part[half:].astype(jnp.bfloat16), bits)
        part = part[:half] + got.astype(jnp.float32)
    return part


def routing_columns(live_counts, expert_ids, gate_scores, experts):
    slots = expert_ids.shape[0]
    live = jnp.arange(slots, dtype=jnp.int32)[:, None] < live_counts[0]
    named = expert_ids[:, :, None] == jnp.arange(experts, dtype=jnp.int32)
    score = jnp.sum(jnp.where(named & live[:, :, None], gate_scores[:, :, None], 0.0), axis=1)
    high = lax.reduce_precision(score, 8, 7)
    low = score - high
    pad = jnp.zeros((slots, -2 * experts % LANES), jnp.float32)
    return jnp.concatenate([high, low, pad], axis=1).astype(jnp.bfloat16)


def load_body(*refs):
    half = len(refs) // 2
    sources, targets, sems = refs[:half], refs[half:-1], refs[-1]
    copies = [
        pltpu.make_async_copy(source, target, sems.at[i])
        for i, (source, target) in enumerate(zip(sources, targets))
    ]
    for copy in copies:
        copy.start()
    for copy in copies:
        copy.wait()


def load_weights(weights):
    return pl.pallas_call(
        load_body,
        in_specs=[pl.BlockSpec(memory_space=pltpu.HBM)] * len(weights),
        out_specs=[pl.BlockSpec(memory_space=pltpu.VMEM)] * len(weights),
        out_shape=[pltpu.VMEM(w.shape, w.dtype) for w in weights],
        scratch_shapes=[pltpu.SemaphoreType.DMA((len(weights),))],
        cost_estimate=pl.CostEstimate(
            flops=10**10, bytes_accessed=2 * sum(w.size for w in weights), transcendentals=0
        ),
        compiler_params=pltpu.CompilerParams(vmem_limit_bytes=2**20),
        name="load",
    )(*weights)


def expert_body(rows, gate_a, up_a, down_a, gate_b, up_b, down_b, out):
    width = out.shape[1]
    inputs = rows[:, :width]
    columns = rows[:, width:].astype(jnp.float32)
    experts = lax.axis_size("expert") // 2
    mine = lax.shift_right_logical(lax.axis_index("expert"), 1)
    lane = lax.broadcasted_iota(jnp.int32, columns.shape, 1)
    named = (lane == mine) | (lane == mine + experts)
    score = jnp.sum(jnp.where(named, columns, 0.0), axis=1, keepdims=True)

    def hidden(gate, up):
        gate_act = jnp.dot(inputs, gate[0], preferred_element_type=jnp.float32)
        up_act = jnp.dot(inputs, up[0], preferred_element_type=jnp.float32)
        return (gate_act / (1.0 + jnp.exp(-gate_act)) * up_act).astype(jnp.bfloat16)

    hidden_a, hidden_b = hidden(gate_a, up_a), hidden(gate_b, up_b)
    step = 512 if width % 512 == 0 else LANES
    for at in range(0, width, step):
        cols = slice(at, at + step)
        value = jnp.dot(hidden_a, down_a[0, :, cols], preferred_element_type=jnp.float32)
        value += jnp.dot(hidden_b, down_b[0, :, cols], preferred_element_type=jnp.float32)
        out[:, cols] = value * score


def expert_rows(rows, weights):
    count, width = rows.shape[0], weights[2].shape[2]
    tile = min(count, 256)
    return pl.pallas_call(
        expert_body,
        grid=(count // tile,),
        in_specs=[
            pl.BlockSpec((tile, rows.shape[1]), lambda i: (i, 0)),
        ]
        + [pl.BlockSpec(memory_space=pltpu.VMEM)] * len(weights),
        out_specs=pl.BlockSpec((tile, width), lambda i: (i, 0)),
        out_shape=jax.ShapeDtypeStruct((count, width), jnp.float32),
        compiler_params=pltpu.CompilerParams(
            dimension_semantics=("arbitrary",), vmem_limit_bytes=24 * 2**20
        ),
        name="experts",
    )(rows, *weights)


def shards(tokens, live_counts, expert_ids, gate_scores, gate_weight, up_weight, down_weight):
    count = lax.axis_size("expert")
    experts = count // 2
    own = (gate_weight, up_weight, down_weight)
    other = [swap(weight, (0, 0)) for weight in own]
    columns = routing_columns(live_counts, expert_ids, gate_scores, experts)
    rows = jnp.concatenate([tokens, columns], axis=1)
    stages = stage_bits(count)
    rows = gather_rows(rows, stages[:-1])
    rows, other = lax.optimization_barrier((rows, other))
    weights = load_weights([*own, *other])
    rows = gather_rows(rows, stages[-1:])
    part = expert_rows(rows, weights)
    return reduce_rows(part, count).astype(jnp.bfloat16)


def solution(mesh):
    in_specs = (
        P(("groups", "expert"), None),
        P(("groups", "expert")),
        P(("groups", "expert"), None),
        P(("groups", "expert"), None),
        P("expert", None, None),
        P("expert", None, None),
        P("expert", None, None),
    )
    out_specs = P(("groups", "expert"), None)
    return jax.shard_map(shards, mesh=mesh, in_specs=in_specs, out_specs=out_specs, check_vma=False)
```

time: 69.7 us -> 60 us (0.86)
  matrix products: 15.3 us -> 0 us
  Pallas kernels: 0 us -> 8.14 us
  waiting for transfers between devices: 35.3 us -> 30.1 us
  local copies, waits for them, and re-layouts: 2.16 us -> 7.34 us
  starting transfers between devices: 14.1 us -> 11.7 us
    dot_general x4 -> x0, matrix products: 15.3 us -> none  [the longest x1 5.37 us: shards(): jnp.dot(far_hidden, down_weight[0], preferred_element_type=jnp.float32)]
    pallas_call x0 -> x2, Pallas kernels: none -> 8.14 us  [the longest x1 4.98 us: load_weights(): pl.pallas_call(load_body, in_specs=[pl.BlockSpec(memory_space=pltpu.HBM)]...]
    unnamed x2 -> x6, local copies, waits for them, and re-layouts: 0.91 us -> 6.11 us
    ppermute x8 -> x9, waiting for transfers between devices: 35.3 us -> 30.1 us  [swap(): return lax.ppermute(block, 'expert', route)]
    ppermute x8 -> x9, starting transfers between devices: 14.1 us -> 11.7 us  [swap(): return lax.ppermute(block, 'expert', route)]
  transfers between devices with their start and end apart: 8 -> 9, of which waited for: 7 -> 5; matrix products, arithmetic and copies ran while one was open for 4% -> 3% of each run, Pallas kernels for 0% -> 8%
where the time goes in v3:
time: 60 us; the launch traced here: 59.7 us
  waiting for transfers between devices  30.1 us (50%)
  starting transfers between devices  11.7 us (20%)
  Pallas kernels  8.14 us (14%)
  local copies, waits for them, and re-layouts  7.34 us (12%)
  other arithmetic  1.65 us (3%)
  between operations  0.77 us (1%)
    ppermute x9, waiting for transfers between devices, swap(): return lax.ppermute(block, 'expert', route)  30.1 us
    ppermute x9, starting transfers between devices, swap(): return lax.ppermute(block, 'expert', route)  11.7 us
    unnamed x6, local copies, waits for them, and re-layouts  6.11 us
    pallas_call x1, Pallas kernels, load_weights(): pl.pallas_call(load_body, in_specs=[pl.BlockSpec(memory_space=pltpu.HBM)]...  4.98 us
    pallas_call x1, Pallas kernels, expert_rows(): pl.pallas_call(expert_body, grid=(count // tile,), in_specs=[pl.BlockSpec...  3.15 us
  transfers between devices with their start and end apart: 9, of which 5 were waited for; matrix products, arithmetic and copies ran while one was open for 3% of the time, Pallas kernels for 8%

profile of v3, /device:TPU:0, one launch (start us, length us, event | category | flops | bytes accessed | tf_op | source)
XLA Modules:
  0.0 59.7 jit_solution(2832548137616697544)
XLA Ops:
  0.0 0.5 collective-permute-start.2
  0.5 0.0 collective-permute-start.3
  0.5 0.5 collective-permute-start.4
  1.7 0.7 %select_reduce_fusion = f32[16,8]{0,1:T(8,128)S(1)} fusion(f32[16,4]{0,1:T(4,128)} %param.10, s32[16,4]{0,1:T(4,128)} %param.9, pred[16]{0:T(512)(128)(4,1)S(1)} %iota_compare_fusion.1), kind=kLoop, calls=%fused_computation.10 | loop fusion | flops 1920 | bytes 1040 | tf_op jit(solution)/shard_map/reduce_sum | solution.py:42
  2.4 0.1 copy.13
  2.5 0.1 copy.12
  2.5 1.0 %concatenate.16 = bf16[16,3712]{1,0:T(8,128)(2,1)S(1)} concatenate(bf16[16,3584]{1,0:T(8,128)(2,1)} %param.7, bf16[16,8]{1,0:T(8,128)(2,1)S(1)} %get-tuple-element.26, bf16[16,8]{1,0:T(8,128)(2,1)S(1)} %get-tuple-element.25, bf16[16,112]{1,0:T(8,128)(2,1)S(1)} %broadcast_in_dim.22), dimensions={1} | concatenate | bytes 237568 | tf_op jit(solution)/shard_map/concatenate | solution.py:126
  3.5 3.6 %collective-permute-start = (bf16[16,3712]{1,0:T(8,128)(2,1)S(1)}, bf16[16,3712]{1,0:T(8,128)(2,1)S(1)}, u32[]{:S(2)}, u32[]{:S(2)}) collective-permute-start(bf16[16,3712]{1,0:T(8,128)(2,1)S(1)} %concatenate.16), channel_id=1, source_target_pairs={{0,8},{1,3},{2,10},{3,1},{4,12},{5,7},{6,14},{7,5},{8,0},{9,11},{1... | collective-permute-start | bytes 356360 | tf_op jit(solution)/shard_map/ppermute | solution.py:21
  7.1 2.8 %collective-permute-done = bf16[16,3712]{1,0:T(8,128)(2,1)S(1)} collective-permute-done((bf16[16,3712]{1,0:T(8,128)(2,1)S(1)}, bf16[16,3712]{1,0:T(8,128)(2,1)S(1)}, u32[]{:S(2)}, u32[]{:S(2)}) %collective-permute-start) | collective-permute-done | bytes 118816 | tf_op jit(solution)/shard_map/ppermute | solution.py:21
  10.0 2.3 %collective-permute-start.1 = (bf16[32,3712]{1,0:T(8,128)(2,1)S(1)}, bf16[32,3712]{1,0:T(8,128)(2,1)S(1)}, u32[]{:S(2)}, u32[]{:S(2)}) collective-permute-start(bf16[32,3712]{1,0:T(8,128)(2,1)S(1)} %pad_maximum_fusion.2), channel_id=1, source_target_pairs={{0,4},{1,9},{2,6},{3,11},{4,0},{5,13},{6,2},{7,15},{8,12},{9,1},{1... | collective-permute-start | bytes 712712 | tf_op jit(solution)/shard_map/ppermute | solution.py:21
  12.3 5.5 %collective-permute-done.1 = bf16[32,3712]{1,0:T(8,128)(2,1)S(1)} collective-permute-done((bf16[32,3712]{1,0:T(8,128)(2,1)S(1)}, bf16[32,3712]{1,0:T(8,128)(2,1)S(1)}, u32[]{:S(2)}, u32[]{:S(2)}) %collective-permute-start.1) | collective-permute-done | bytes 237600 | tf_op jit(solution)/shard_map/ppermute | solution.py:21
  17.8 0.0 collective-permute-done.2.refs_3_
  17.8 0.0 collective-permute-done.3.refs_4_
  17.8 0.0 collective-permute-done.4.refs_5_
  17.8 3.0 %collective-permute-start.5 = (bf16[64,3712]{1,0:T(8,128)(2,1)S(1)}, bf16[64,3712]{1,0:T(8,128)(2,1)S(1)}, u32[]{:S(2)}, u32[]{:S(2)}) collective-permute-start(bf16[64,3712]{1,0:T(8,128)(2,1)S(1)} %pad_maximum_fusion.1), channel_id=1, source_target_pairs={{0,2},{1,5},{2,0},{3,7},{4,6},{5,1},{6,4},{7,3},{8,10},{9,13},{10,... | collective-permute-start | bytes 1425416 | tf_op jit(solution)/shard_map/ppermute | solution.py:21
  20.8 0.0 copy-start
  20.8 2.0 %copy-done = bf16[1,3584,512]{2,1,0:T(8,128)(2,1)S(1)} copy-done((bf16[1,3584,512]{2,1,0:T(8,128)(2,1)S(1)}, bf16[1,3584,512]{2,1,0:T(8,128)(2,1)}, u32[]{:S(2)}) %copy-start) | copy-done | bytes 3670040
  22.8 0.0 copy-start.1
  22.8 2.0 %copy-done.1 = bf16[1,3584,512]{2,1,0:T(8,128)(2,1)S(1)} copy-done((bf16[1,3584,512]{2,1,0:T(8,128)(2,1)S(1)}, bf16[1,3584,512]{2,1,0:T(8,128)(2,1)}, u32[]{:S(2)}) %copy-start.1) | copy-done | bytes 3670040
  24.9 0.0 copy-start.2
  24.9 2.0 %copy-done.2 = bf16[1,512,3584]{2,1,0:T(8,128)(2,1)S(1)} copy-done((bf16[1,512,3584]{2,1,0:T(8,128)(2,1)S(1)}, bf16[1,512,3584]{2,1,0:T(8,128)(2,1)}, u32[]{:S(2)}) %copy-start.2) | copy-done | bytes 3670040
  26.9 5.0 %load.1 = (bf16[1,3584,512]{2,1,0:T(8,128)(2,1)S(1)}, bf16[1,3584,512]{2,1,0:T(8,128)(2,1)S(1)}, bf16[1,512,3584]{2,1,0:T(8,128)(2,1)S(1)}, bf16[1,3584,512]{2,1...) custom-call(bf16[1,3584,512]{2,1,0:T(8,128)(2,1)S(1)} %copy-done, ...), custom_call_target="tpu_custom_call" | custom-call | flops 10000000000 | bytes 22020096 | tf_op jit(solution)/shard_map/load/pallas_call | solution.py:63
  31.9 0.0 collective-permute-done.5
  31.9 0.1 pad_maximum_fusion.rows
  32.0 3.2 %experts.1 = f32[128,3584]{1,0:T(8,128)S(1)} custom-call(bf16[128,3712]{1,0:T(8,128)(2,1)S(1)} %pad_maximum_fusion.rows, bf16[1,3584,512]{2,1,0:T(8,128)(2,1)S(1)} %get-tuple-element.19.gate_a, bf16[1,3584,512]{2,1,0:T(8,128)(2,1)S(1)} %get-tuple-element.20.up_a, bf16[1,512,3584]{2,1,0:T(8,128)(2,1)S(1)} %get-tuple-element.21.down_a, ...), custom_call_target="tpu_custom_call" | custom-call | tf_op jit(solution)/shard_map/experts/pallas_call | solution.py:104
  35.2 0.1 collective-permute-start.6
  35.3 8.5 %collective-permute-done.6 = bf16[64,3584]{1,0:T(8,128)(2,1)S(1)} collective-permute-done((bf16[64,3584]{1,0:T(8,128)(2,1)S(1)}, bf16[64,3584]{1,0:T(8,128)(2,1)S(1)}, u32[]{:S(2)}, u32[]{:S(2)}) %collective-permute-start.6) | collective-permute-done | bytes 458784 | tf_op jit(solution)/shard_map/ppermute | solution.py:21
  43.8 0.1 slice_add_fusion
  43.9 1.1 %collective-permute-start.7 = (bf16[32,3584]{1,0:T(8,128)(2,1)S(1)}, bf16[32,3584]{1,0:T(8,128)(2,1)S(1)}, u32[]{:S(2)}, u32[]{:S(2)}) collective-permute-start(bf16[32,3584]{1,0:T(8,128)(2,1)S(1)} %slice.42), channel_id=1, source_target_pairs={{0,4},{1,9},{2,6},{3,11},{4,0},{5,13},{6,2},{7,15},{8,12},{9,1},{1... | collective-permute-start | bytes 688136 | tf_op jit(solution)/shard_map/ppermute | solution.py:21
  44.9 7.4 %collective-permute-done.7 = bf16[32,3584]{1,0:T(8,128)(2,1)S(1)} collective-permute-done((bf16[32,3584]{1,0:T(8,128)(2,1)S(1)}, bf16[32,3584]{1,0:T(8,128)(2,1)S(1)}, u32[]{:S(2)}, u32[]{:S(2)}) %collective-permute-start.7) | collective-permute-done | bytes 229408 | tf_op jit(solution)/shard_map/ppermute | solution.py:21
  52.3 0.1 slice_add_fusion.1
  52.4 0.7 %collective-permute-start.8 = (bf16[16,3584]{1,0:T(8,128)(2,1)S(1)}, bf16[16,3584]{1,0:T(8,128)(2,1)S(1)}, u32[]{:S(2)}, u32[]{:S(2)}) collective-permute-start(bf16[16,3584]{1,0:T(8,128)(2,1)S(1)} %slice.43), channel_id=1, source_target_pairs={{0,8},{1,3},{2,10},{3,1},{4,12},{5,7},{6,14},{7,5},{8,0},{9,11},{1... | collective-permute-start | bytes 344072 | tf_op jit(solution)/shard_map/ppermute | solution.py:21
  53.1 6.0 %collective-permute-done.8 = bf16[16,3584]{1,0:T(8,128)(2,1)S(1)} collective-permute-done((bf16[16,3584]{1,0:T(8,128)(2,1)S(1)}, bf16[16,3584]{1,0:T(8,128)(2,1)S(1)}, u32[]{:S(2)}, u32[]{:S(2)}) %collective-permute-start.8) | collective-permute-done | bytes 114720 | tf_op jit(solution)/shard_map/ppermute | solution.py:21
  59.0 0.7 %fusion = bf16[16,3584]{1,0:T(8,128)(2,1)} fusion(f32[32,3584]{1,0:T(8,128)S(1)} %slice_add_fusion.1, bf16[16,3584]{1,0:T(8,128)(2,1)S(1)} %collective-permute-done.8), kind=kLoop, calls=%fused_computation.9 | loop fusion | flops 172032 | bytes 458752 | tf_op jit(solution)/shard_map/convert_element_type | solution.py:133
  (9 shorter events, 0.2 us)
Async XLA Ops:
  0.0 17.8 %collective-permute-start.2 = (bf16[1,3584,512]{2,1,0:T(8,128)(2,1)}, bf16[1,3584,512]{2,1,0:T(8,128)(2,1)}, u32[]{:S(2)}, u32[]{:S(2)}) collective-permute-start(bf16[1,3584,512]{2,1,0:T(8,128)(2,1)} %refs_0_.1), channel_id=1, source_target_pairs={{0,1},{1,0},{2,3},{3,2},{4,5},{5,4},{6,7},{7,6},{8,9},{9,8},{10,11... | collective-permute-start | bytes 11010056 | tf_op jit(solution)/shard_map/ppermute | solution.py:21
  0.5 17.3 %collective-permute-start.3 = (bf16[1,3584,512]{2,1,0:T(8,128)(2,1)}, bf16[1,3584,512]{2,1,0:T(8,128)(2,1)}, u32[]{:S(2)}, u32[]{:S(2)}) collective-permute-start(bf16[1,3584,512]{2,1,0:T(8,128)(2,1)} %refs_1_.1), channel_id=1, source_target_pairs={{0,1},{1,0},{2,3},{3,2},{4,5},{5,4},{6,7},{7,6},{8,9},{9,8},{10,11... | collective-permute-start | bytes 11010056 | tf_op jit(solution)/shard_map/ppermute | solution.py:21
  0.5 17.3 %collective-permute-start.4 = (bf16[1,512,3584]{2,1,0:T(8,128)(2,1)}, bf16[1,512,3584]{2,1,0:T(8,128)(2,1)}, u32[]{:S(2)}, u32[]{:S(2)}) collective-permute-start(bf16[1,512,3584]{2,1,0:T(8,128)(2,1)} %refs_2_.1), channel_id=1, source_target_pairs={{0,1},{1,0},{2,3},{3,2},{4,5},{5,4},{6,7},{7,6},{8,9},{9,8},{10,11... | collective-permute-start | bytes 11010056 | tf_op jit(solution)/shard_map/ppermute | solution.py:21
  3.5 6.4 %collective-permute-start = (bf16[16,3712]{1,0:T(8,128)(2,1)S(1)}, bf16[16,3712]{1,0:T(8,128)(2,1)S(1)}, u32[]{:S(2)}, u32[]{:S(2)}) collective-permute-start(bf16[16,3712]{1,0:T(8,128)(2,1)S(1)} %concatenate.16), channel_id=1, source_target_pairs={{0,8},{1,3},{2,10},{3,1},{4,12},{5,7},{6,14},{7,5},{8,0},{9,11},{1... | collective-permute-start | bytes 356360 | tf_op jit(solution)/shard_map/ppermute | solution.py:21
  10.0 7.8 %collective-permute-start.1 = (bf16[32,3712]{1,0:T(8,128)(2,1)S(1)}, bf16[32,3712]{1,0:T(8,128)(2,1)S(1)}, u32[]{:S(2)}, u32[]{:S(2)}) collective-permute-start(bf16[32,3712]{1,0:T(8,128)(2,1)S(1)} %pad_maximum_fusion.2), channel_id=1, source_target_pairs={{0,4},{1,9},{2,6},{3,11},{4,0},{5,13},{6,2},{7,15},{8,12},{9,1},{1... | collective-permute-start | bytes 712712 | tf_op jit(solution)/shard_map/ppermute | solution.py:21
  17.8 14.1 %collective-permute-start.5 = (bf16[64,3712]{1,0:T(8,128)(2,1)S(1)}, bf16[64,3712]{1,0:T(8,128)(2,1)S(1)}, u32[]{:S(2)}, u32[]{:S(2)}) collective-permute-start(bf16[64,3712]{1,0:T(8,128)(2,1)S(1)} %pad_maximum_fusion.1), channel_id=1, source_target_pairs={{0,2},{1,5},{2,0},{3,7},{4,6},{5,1},{6,4},{7,3},{8,10},{9,13},{10,... | collective-permute-start | bytes 1425416 | tf_op jit(solution)/shard_map/ppermute | solution.py:21
  20.8 2.0 %copy-start = (bf16[1,3584,512]{2,1,0:T(8,128)(2,1)S(1)}, bf16[1,3584,512]{2,1,0:T(8,128)(2,1)}, u32[]{:S(2)}) copy-start(bf16[1,3584,512]{2,1,0:T(8,128)(2,1)} %refs_0_.1) | copy-start | bytes 11010052
  22.8 2.0 %copy-start.1 = (bf16[1,3584,512]{2,1,0:T(8,128)(2,1)S(1)}, bf16[1,3584,512]{2,1,0:T(8,128)(2,1)}, u32[]{:S(2)}) copy-start(bf16[1,3584,512]{2,1,0:T(8,128)(2,1)} %refs_1_.1) | copy-start | bytes 11010052
  24.9 2.0 %copy-start.2 = (bf16[1,512,3584]{2,1,0:T(8,128)(2,1)S(1)}, bf16[1,512,3584]{2,1,0:T(8,128)(2,1)}, u32[]{:S(2)}) copy-start(bf16[1,512,3584]{2,1,0:T(8,128)(2,1)} %refs_2_.1) | copy-start | bytes 11010052
  35.2 8.5 %collective-permute-start.6 = (bf16[64,3584]{1,0:T(8,128)(2,1)S(1)}, bf16[64,3584]{1,0:T(8,128)(2,1)S(1)}, u32[]{:S(2)}, u32[]{:S(2)}) collective-permute-start(bf16[64,3584]{1,0:T(8,128)(2,1)S(1)} %slice.41), channel_id=1, source_target_pairs={{0,2},{1,5},{2,0},{3,7},{4,6},{5,1},{6,4},{7,3},{8,10},{9,13},{10,... | collective-permute-start | bytes 1376264 | tf_op jit(solution)/shard_map/ppermute | solution.py:21
  43.9 8.4 %collective-permute-start.7 = (bf16[32,3584]{1,0:T(8,128)(2,1)S(1)}, bf16[32,3584]{1,0:T(8,128)(2,1)S(1)}, u32[]{:S(2)}, u32[]{:S(2)}) collective-permute-start(bf16[32,3584]{1,0:T(8,128)(2,1)S(1)} %slice.42), channel_id=1, source_target_pairs={{0,4},{1,9},{2,6},{3,11},{4,0},{5,13},{6,2},{7,15},{8,12},{9,1},{1... | collective-permute-start | bytes 688136 | tf_op jit(solution)/shard_map/ppermute | solution.py:21
  52.4 6.7 %collective-permute-start.8 = (bf16[16,3584]{1,0:T(8,128)(2,1)S(1)}, bf16[16,3584]{1,0:T(8,128)(2,1)S(1)}, u32[]{:S(2)}, u32[]{:S(2)}) collective-permute-start(bf16[16,3584]{1,0:T(8,128)(2,1)S(1)} %slice.43), channel_id=1, source_target_pairs={{0,8},{1,3},{2,10},{3,1},{4,12},{5,7},{6,14},{7,5},{8,0},{9,11},{1... | collective-permute-start | bytes 344072 | tf_op jit(solution)/shard_map/ppermute | solution.py:21

commit v4 on v3

--- a/solution.py
+++ b/solution.py
@@ -67,7 +67,7 @@
         out_shape=[pltpu.VMEM(w.shape, w.dtype) for w in weights],
         scratch_shapes=[pltpu.SemaphoreType.DMA((len(weights),))],
         cost_estimate=pl.CostEstimate(
-            flops=10**10, bytes_accessed=2 * sum(w.size for w in weights), transcendentals=0
+            flops=10**10, bytes_accessed=0, transcendentals=0
         ),
         compiler_params=pltpu.CompilerParams(vmem_limit_bytes=2**20),
         name="load",
@@ -125,11 +125,14 @@
     columns = routing_columns(live_counts, expert_ids, gate_scores, experts)
     rows = jnp.concatenate([tokens, columns], axis=1)
     stages = stage_bits(count)
-    rows = gather_rows(rows, stages[:-1])
-    rows, other = lax.optimization_barrier((rows, other))
-    weights = load_weights([*own, *other])
+    rows = gather_rows(rows, stages[:-2])
+    own = lax.optimization_barrier((rows, own))[1]
+    own = load_weights(own)
+    rows = gather_rows(rows, stages[-2:-1])
+    other = lax.optimization_barrier((rows, other))[1]
+    other = load_weights(other)
     rows = gather_rows(rows, stages[-1:])
-    part = expert_rows(rows, weights)
+    part = expert_rows(rows, [*own, *other])
     return reduce_rows(part, count).astype(jnp.bfloat16)
 
 

time: 60 us -> 59.7 us (level)
  waiting for transfers between devices: 30.1 us -> 28.1 us
  starting transfers between devices: 11.7 us -> 13.4 us
    ppermute x9, waiting for transfers between devices: 30.1 us -> 28.1 us  [swap(): return lax.ppermute(block, 'expert', route)]
    ppermute x9, starting transfers between devices: 11.7 us -> 13.4 us  [swap(): return lax.ppermute(block, 'expert', route)]
    pallas_call x1 -> x2, Pallas kernels: 4.98 us -> 4.99 us  [load_weights(): pl.pallas_call(load_body, in_specs=[pl.BlockSpec(memory_space=pltpu.HBM)]...]
  transfers between devices with their start and end apart: 9 -> 9, of which waited for: 5 -> 5; matrix products, arithmetic and copies ran while one was open for 3% -> 3% of each run, Pallas kernels for 8% -> 1%
where the time goes in v4:
time: 59.7 us; the launch traced here: 59.5 us
  waiting for transfers between devices  28.1 us (47%)
  starting transfers between devices  13.4 us (22%)
  Pallas kernels  8.15 us (14%)
  local copies, waits for them, and re-layouts  7.34 us (12%)
  other arithmetic  1.68 us (3%)
  between operations  0.77 us (1%)
    ppermute x9, waiting for transfers between devices, swap(): return lax.ppermute(block, 'expert', route)  28.1 us
    ppermute x9, starting transfers between devices, swap(): return lax.ppermute(block, 'expert', route)  13.4 us
    unnamed x6, local copies, waits for them, and re-layouts  6.11 us
    pallas_call x2, Pallas kernels, load_weights(): pl.pallas_call(load_body, in_specs=[pl.BlockSpec(memory_space=pltpu.HBM)]...  4.99 us
    pallas_call x1, Pallas kernels, expert_rows(): pl.pallas_call(expert_body, grid=(count // tile,), in_specs=[pl.BlockSpec...  3.16 us
  transfers between devices with their start and end apart: 9, of which 5 were waited for; matrix products, arithmetic and copies ran while one was open for 3% of the time, Pallas kernels for 1%

profile of v4, /device:TPU:0, one launch (start us, length us, event | category | flops | bytes accessed | tf_op | source)
XLA Modules:
  0.0 59.5 jit_solution(10824609976130430878)
XLA Ops:
  0.0 0.5 collective-permute-start.3
  0.5 0.0 collective-permute-start.4
  0.5 0.5 collective-permute-start.5
  1.7 0.7 %select_reduce_fusion = f32[16,8]{0,1:T(8,128)S(1)} fusion(f32[16,4]{0,1:T(4,128)} %param.10, s32[16,4]{0,1:T(4,128)} %param.9, pred[16]{0:T(512)(128)(4,1)S(1)} %iota_compare_fusion.1), kind=kLoop, calls=%fused_computation.10 | loop fusion | flops 1920 | bytes 1040 | tf_op jit(solution)/shard_map/reduce_sum | solution.py:42
  2.4 0.1 copy.13
  2.5 0.1 copy.12
  2.5 1.0 %concatenate.17 = bf16[16,3712]{1,0:T(8,128)(2,1)S(1)} concatenate(bf16[16,3584]{1,0:T(8,128)(2,1)} %param.7, bf16[16,8]{1,0:T(8,128)(2,1)S(1)} %get-tuple-element.30, bf16[16,8]{1,0:T(8,128)(2,1)S(1)} %get-tuple-element.29, bf16[16,112]{1,0:T(8,128)(2,1)S(1)} %broadcast_in_dim.22), dimensions={1} | concatenate | bytes 237568 | tf_op jit(solution)/shard_map/concatenate | solution.py:126
  3.5 3.6 %collective-permute-start = (bf16[16,3712]{1,0:T(8,128)(2,1)S(1)}, bf16[16,3712]{1,0:T(8,128)(2,1)S(1)}, u32[]{:S(2)}, u32[]{:S(2)}) collective-permute-start(bf16[16,3712]{1,0:T(8,128)(2,1)S(1)} %concatenate.17), channel_id=1, source_target_pairs={{0,8},{1,3},{2,10},{3,1},{4,12},{5,7},{6,14},{7,5},{8,0},{9,11},{1... | collective-permute-start | bytes 356360 | tf_op jit(solution)/shard_map/ppermute | solution.py:21
  7.1 2.8 %collective-permute-done = bf16[16,3712]{1,0:T(8,128)(2,1)S(1)} collective-permute-done((bf16[16,3712]{1,0:T(8,128)(2,1)S(1)}, bf16[16,3712]{1,0:T(8,128)(2,1)S(1)}, u32[]{:S(2)}, u32[]{:S(2)}) %collective-permute-start) | collective-permute-done | bytes 118816 | tf_op jit(solution)/shard_map/ppermute | solution.py:21
  10.0 2.3 %collective-permute-start.1 = (bf16[32,3712]{1,0:T(8,128)(2,1)S(1)}, bf16[32,3712]{1,0:T(8,128)(2,1)S(1)}, u32[]{:S(2)}, u32[]{:S(2)}) collective-permute-start(bf16[32,3712]{1,0:T(8,128)(2,1)S(1)} %pad_maximum_fusion.2), channel_id=1, source_target_pairs={{0,4},{1,9},{2,6},{3,11},{4,0},{5,13},{6,2},{7,15},{8,12},{9,1},{1... | collective-permute-start | bytes 712712 | tf_op jit(solution)/shard_map/ppermute | solution.py:21
  12.3 5.5 %collective-permute-done.1 = bf16[32,3712]{1,0:T(8,128)(2,1)S(1)} collective-permute-done((bf16[32,3712]{1,0:T(8,128)(2,1)S(1)}, bf16[32,3712]{1,0:T(8,128)(2,1)S(1)}, u32[]{:S(2)}, u32[]{:S(2)}) %collective-permute-start.1) | collective-permute-done | bytes 237600 | tf_op jit(solution)/shard_map/ppermute | solution.py:21
  17.8 3.0 %collective-permute-start.2 = (bf16[64,3712]{1,0:T(8,128)(2,1)S(1)}, bf16[64,3712]{1,0:T(8,128)(2,1)S(1)}, u32[]{:S(2)}, u32[]{:S(2)}) collective-permute-start(bf16[64,3712]{1,0:T(8,128)(2,1)S(1)} %pad_maximum_fusion.1), channel_id=1, source_target_pairs={{0,2},{1,5},{2,0},{3,7},{4,6},{5,1},{6,4},{7,3},{8,10},{9,13},{10,... | collective-permute-start | bytes 1425416 | tf_op jit(solution)/shard_map/ppermute | solution.py:21
  20.8 0.0 copy-start
  20.8 2.0 %copy-done = bf16[1,3584,512]{2,1,0:T(8,128)(2,1)S(1)} copy-done((bf16[1,3584,512]{2,1,0:T(8,128)(2,1)S(1)}, bf16[1,3584,512]{2,1,0:T(8,128)(2,1)}, u32[]{:S(2)}) %copy-start) | copy-done | bytes 3670040
  22.8 0.0 copy-start.1
  22.8 2.0 %copy-done.1 = bf16[1,3584,512]{2,1,0:T(8,128)(2,1)S(1)} copy-done((bf16[1,3584,512]{2,1,0:T(8,128)(2,1)S(1)}, bf16[1,3584,512]{2,1,0:T(8,128)(2,1)}, u32[]{:S(2)}) %copy-start.1) | copy-done | bytes 3670040
  24.8 0.0 copy-start.2
  24.9 2.0 %copy-done.2 = bf16[1,512,3584]{2,1,0:T(8,128)(2,1)S(1)} copy-done((bf16[1,512,3584]{2,1,0:T(8,128)(2,1)S(1)}, bf16[1,512,3584]{2,1,0:T(8,128)(2,1)}, u32[]{:S(2)}) %copy-start.2) | copy-done | bytes 3670040
  26.9 0.8 %load.2 = (bf16[1,3584,512]{2,1,0:T(8,128)(2,1)S(1)}, bf16[1,3584,512]{2,1,0:T(8,128)(2,1)S(1)}, bf16[1,512,3584]{2,1,0:T(8,128)(2,1)S(1)}) custom-call(bf16[1,3584,512]{2,1,0:T(8,128)(2,1)S(1)} %copy-done, bf16[1,3584,512]{2,1,0:T(8,128)(2,1)S(1)} %copy-done.1, bf16[1,512,3584]{2,1,0:T(8,128)(2,1)S(1)} %copy-done.2), custom_call_target="tpu_custom_call" | custom-call | flops 10000000000 | tf_op jit(solution)/shard_map/load/pallas_call | solution.py:63
  27.7 0.0 collective-permute-done.2
  27.7 0.1 pad_maximum_fusion.rows
  27.8 0.0 collective-permute-done.3.refs_0_
  27.8 0.0 collective-permute-done.4.refs_1_
  27.8 0.0 collective-permute-done.5.refs_2_
  27.8 4.2 %load.3 = (bf16[1,3584,512]{2,1,0:T(8,128)(2,1)S(1)}, bf16[1,3584,512]{2,1,0:T(8,128)(2,1)S(1)}, bf16[1,512,3584]{2,1,0:T(8,128)(2,1)S(1)}) custom-call(bf16[1,3584,512]{2,1,0:T(8,128)(2,1)} %collective-permute-done.3.refs_0_, bf16[1,3584,512]{2,1,0:T(8,128)(2,1)} %collective-permute-done.4.refs_1_, bf16[1,512,3584]{2,1,0:T(8,128)(2,1)} %collective-permute-done.5.refs_2_), custom_call_target="tpu_custom_call" | custom-call | flops 10000000000 | tf_op jit(solution)/shard_map/load/pallas_call | solution.py:63
  32.0 3.2 %experts.1 = f32[128,3584]{1,0:T(8,128)S(1)} custom-call(bf16[128,3712]{1,0:T(8,128)(2,1)S(1)} %pad_maximum_fusion.rows, bf16[1,3584,512]{2,1,0:T(8,128)(2,1)S(1)} %get-tuple-element.20.gate_a, bf16[1,3584,512]{2,1,0:T(8,128)(2,1)S(1)} %get-tuple-element.21.up_a, bf16[1,512,3584]{2,1,0:T(8,128)(2,1)S(1)} %get-tuple-element.22.down_a, ...), custom_call_target="tpu_custom_call" | custom-call | tf_op jit(solution)/shard_map/experts/pallas_call | solution.py:104
  35.2 1.8 %collective-permute-start.6 = (bf16[64,3584]{1,0:T(8,128)(2,1)S(1)}, bf16[64,3584]{1,0:T(8,128)(2,1)S(1)}, u32[]{:S(2)}, u32[]{:S(2)}) collective-permute-start(bf16[64,3584]{1,0:T(8,128)(2,1)S(1)} %slice.41), channel_id=1, source_target_pairs={{0,2},{1,5},{2,0},{3,7},{4,6},{5,1},{6,4},{7,3},{8,10},{9,13},{10,... | collective-permute-start | bytes 1376264 | tf_op jit(solution)/shard_map/ppermute | solution.py:21
  37.1 6.7 %collective-permute-done.6 = bf16[64,3584]{1,0:T(8,128)(2,1)S(1)} collective-permute-done((bf16[64,3584]{1,0:T(8,128)(2,1)S(1)}, bf16[64,3584]{1,0:T(8,128)(2,1)S(1)}, u32[]{:S(2)}, u32[]{:S(2)}) %collective-permute-start.6) | collective-permute-done | bytes 458784 | tf_op jit(solution)/shard_map/ppermute | solution.py:21
  43.8 0.1 slice_add_fusion
  43.9 0.3 collective-permute-start.7
  44.2 7.6 %collective-permute-done.7 = bf16[32,3584]{1,0:T(8,128)(2,1)S(1)} collective-permute-done((bf16[32,3584]{1,0:T(8,128)(2,1)S(1)}, bf16[32,3584]{1,0:T(8,128)(2,1)S(1)}, u32[]{:S(2)}, u32[]{:S(2)}) %collective-permute-start.7) | collective-permute-done | bytes 229408 | tf_op jit(solution)/shard_map/ppermute | solution.py:21
  51.7 0.1 slice_add_fusion.1
  51.8 1.4 %collective-permute-start.8 = (bf16[16,3584]{1,0:T(8,128)(2,1)S(1)}, bf16[16,3584]{1,0:T(8,128)(2,1)S(1)}, u32[]{:S(2)}, u32[]{:S(2)}) collective-permute-start(bf16[16,3584]{1,0:T(8,128)(2,1)S(1)} %slice.43), channel_id=1, source_target_pairs={{0,8},{1,3},{2,10},{3,1},{4,12},{5,7},{6,14},{7,5},{8,0},{9,11},{1... | collective-permute-start | bytes 344072 | tf_op jit(solution)/shard_map/ppermute | solution.py:21
  53.2 5.5 %collective-permute-done.8 = bf16[16,3584]{1,0:T(8,128)(2,1)S(1)} collective-permute-done((bf16[16,3584]{1,0:T(8,128)(2,1)S(1)}, bf16[16,3584]{1,0:T(8,128)(2,1)S(1)}, u32[]{:S(2)}, u32[]{:S(2)}) %collective-permute-start.8) | collective-permute-done | bytes 114720 | tf_op jit(solution)/shard_map/ppermute | solution.py:21
  58.8 0.7 %fusion = bf16[16,3584]{1,0:T(8,128)(2,1)} fusion(f32[32,3584]{1,0:T(8,128)S(1)} %slice_add_fusion.1, bf16[16,3584]{1,0:T(8,128)(2,1)S(1)} %collective-permute-done.8), kind=kLoop, calls=%fused_computation.9 | loop fusion | flops 172032 | bytes 458752 | tf_op jit(solution)/shard_map/convert_element_type | solution.py:136
  (9 shorter events, 0.2 us)
Async XLA Ops:
  0.0 27.8 %collective-permute-start.3 = (bf16[1,3584,512]{2,1,0:T(8,128)(2,1)}, bf16[1,3584,512]{2,1,0:T(8,128)(2,1)}, u32[]{:S(2)}, u32[]{:S(2)}) collective-permute-start(bf16[1,3584,512]{2,1,0:T(8,128)(2,1)} %refs_0_), channel_id=1, source_target_pairs={{0,1},{1,0},{2,3},{3,2},{4,5},{5,4},{6,7},{7,6},{8,9},{9,8},{10,11... | collective-permute-start | bytes 11010056 | tf_op jit(solution)/shard_map/ppermute | solution.py:21
  0.5 27.3 %collective-permute-start.4 = (bf16[1,3584,512]{2,1,0:T(8,128)(2,1)}, bf16[1,3584,512]{2,1,0:T(8,128)(2,1)}, u32[]{:S(2)}, u32[]{:S(2)}) collective-permute-start(bf16[1,3584,512]{2,1,0:T(8,128)(2,1)} %refs_1_), channel_id=1, source_target_pairs={{0,1},{1,0},{2,3},{3,2},{4,5},{5,4},{6,7},{7,6},{8,9},{9,8},{10,11... | collective-permute-start | bytes 11010056 | tf_op jit(solution)/shard_map/ppermute | solution.py:21
  0.5 27.3 %collective-permute-start.5 = (bf16[1,512,3584]{2,1,0:T(8,128)(2,1)}, bf16[1,512,3584]{2,1,0:T(8,128)(2,1)}, u32[]{:S(2)}, u32[]{:S(2)}) collective-permute-start(bf16[1,512,3584]{2,1,0:T(8,128)(2,1)} %refs_2_), channel_id=1, source_target_pairs={{0,1},{1,0},{2,3},{3,2},{4,5},{5,4},{6,7},{7,6},{8,9},{9,8},{10,11... | collective-permute-start | bytes 11010056 | tf_op jit(solution)/shard_map/ppermute | solution.py:21
  3.5 6.4 %collective-permute-start = (bf16[16,3712]{1,0:T(8,128)(2,1)S(1)}, bf16[16,3712]{1,0:T(8,128)(2,1)S(1)}, u32[]{:S(2)}, u32[]{:S(2)}) collective-permute-start(bf16[16,3712]{1,0:T(8,128)(2,1)S(1)} %concatenate.17), channel_id=1, source_target_pairs={{0,8},{1,3},{2,10},{3,1},{4,12},{5,7},{6,14},{7,5},{8,0},{9,11},{1... | collective-permute-start | bytes 356360 | tf_op jit(solution)/shard_map/ppermute | solution.py:21
  10.0 7.8 %collective-permute-start.1 = (bf16[32,3712]{1,0:T(8,128)(2,1)S(1)}, bf16[32,3712]{1,0:T(8,128)(2,1)S(1)}, u32[]{:S(2)}, u32[]{:S(2)}) collective-permute-start(bf16[32,3712]{1,0:T(8,128)(2,1)S(1)} %pad_maximum_fusion.2), channel_id=1, source_target_pairs={{0,4},{1,9},{2,6},{3,11},{4,0},{5,13},{6,2},{7,15},{8,12},{9,1},{1... | collective-permute-start | bytes 712712 | tf_op jit(solution)/shard_map/ppermute | solution.py:21
  17.8 9.8 %collective-permute-start.2 = (bf16[64,3712]{1,0:T(8,128)(2,1)S(1)}, bf16[64,3712]{1,0:T(8,128)(2,1)S(1)}, u32[]{:S(2)}, u32[]{:S(2)}) collective-permute-start(bf16[64,3712]{1,0:T(8,128)(2,1)S(1)} %pad_maximum_fusion.1), channel_id=1, source_target_pairs={{0,2},{1,5},{2,0},{3,7},{4,6},{5,1},{6,4},{7,3},{8,10},{9,13},{10,... | collective-permute-start | bytes 1425416 | tf_op jit(solution)/shard_map/ppermute | solution.py:21
  20.8 2.0 %copy-start = (bf16[1,3584,512]{2,1,0:T(8,128)(2,1)S(1)}, bf16[1,3584,512]{2,1,0:T(8,128)(2,1)}, u32[]{:S(2)}) copy-start(bf16[1,3584,512]{2,1,0:T(8,128)(2,1)} %refs_0_) | copy-start | bytes 11010052
  22.8 2.0 %copy-start.1 = (bf16[1,3584,512]{2,1,0:T(8,128)(2,1)S(1)}, bf16[1,3584,512]{2,1,0:T(8,128)(2,1)}, u32[]{:S(2)}) copy-start(bf16[1,3584,512]{2,1,0:T(8,128)(2,1)} %refs_1_) | copy-start | bytes 11010052
  24.8 2.0 %copy-start.2 = (bf16[1,512,3584]{2,1,0:T(8,128)(2,1)S(1)}, bf16[1,512,3584]{2,1,0:T(8,128)(2,1)}, u32[]{:S(2)}) copy-start(bf16[1,512,3584]{2,1,0:T(8,128)(2,1)} %refs_2_) | copy-start | bytes 11010052
  35.2 8.5 %collective-permute-start.6 = (bf16[64,3584]{1,0:T(8,128)(2,1)S(1)}, bf16[64,3584]{1,0:T(8,128)(2,1)S(1)}, u32[]{:S(2)}, u32[]{:S(2)}) collective-permute-start(bf16[64,3584]{1,0:T(8,128)(2,1)S(1)} %slice.41), channel_id=1, source_target_pairs={{0,2},{1,5},{2,0},{3,7},{4,6},{5,1},{6,4},{7,3},{8,10},{9,13},{10,... | collective-permute-start | bytes 1376264 | tf_op jit(solution)/shard_map/ppermute | solution.py:21
  43.9 7.8 %collective-permute-start.7 = (bf16[32,3584]{1,0:T(8,128)(2,1)S(1)}, bf16[32,3584]{1,0:T(8,128)(2,1)S(1)}, u32[]{:S(2)}, u32[]{:S(2)}) collective-permute-start(bf16[32,3584]{1,0:T(8,128)(2,1)S(1)} %slice.42), channel_id=1, source_target_pairs={{0,4},{1,9},{2,6},{3,11},{4,0},{5,13},{6,2},{7,15},{8,12},{9,1},{1... | collective-permute-start | bytes 688136 | tf_op jit(solution)/shard_map/ppermute | solution.py:21
  51.8 7.0 %collective-permute-start.8 = (bf16[16,3584]{1,0:T(8,128)(2,1)S(1)}, bf16[16,3584]{1,0:T(8,128)(2,1)S(1)}, u32[]{:S(2)}, u32[]{:S(2)}) collective-permute-start(bf16[16,3584]{1,0:T(8,128)(2,1)S(1)} %slice.43), channel_id=1, source_target_pairs={{0,8},{1,3},{2,10},{3,1},{4,12},{5,7},{6,14},{7,5},{8,0},{9,11},{1... | collective-permute-start | bytes 344072 | tf_op jit(solution)/shard_map/ppermute | solution.py:21

commit v5 on v4

--- a/solution.py
+++ b/solution.py
@@ -126,10 +126,10 @@
     rows = jnp.concatenate([tokens, columns], axis=1)
     stages = stage_bits(count)
     rows = gather_rows(rows, stages[:-2])
-    own = lax.optimization_barrier((rows, own))[1]
+    rows, own = lax.optimization_barrier((rows, own))
     own = load_weights(own)
     rows = gather_rows(rows, stages[-2:-1])
-    other = lax.optimization_barrier((rows, other))[1]
+    rows, other = lax.optimization_barrier((rows, other))
     other = load_weights(other)
     rows = gather_rows(rows, stages[-1:])
     part = expert_rows(rows, [*own, *other])

time: 59.7 us -> 54.1 us (0.906)
  waiting for transfers between devices: 28.1 us -> 22.1 us
    ppermute x9, waiting for transfers between devices: 28.1 us -> 22.1 us  [swap(): return lax.ppermute(block, 'expert', route)]
  transfers between devices with their start and end apart: 9 -> 9, of which waited for: 5 -> 5; matrix products, arithmetic and copies ran while one was open for 3% -> 4% of each run, Pallas kernels for 1% -> 9%
where the time goes in v5:
time: 54.1 us; the launch traced here: 53.8 us
  waiting for transfers between devices  22.1 us (41%)
  starting transfers between devices  13.8 us (26%)
  Pallas kernels  8.14 us (15%)
  local copies, waits for them, and re-layouts  7.34 us (14%)
  other arithmetic  1.65 us (3%)
  between operations  0.78 us (1%)
    ppermute x9, waiting for transfers between devices, swap(): return lax.ppermute(block, 'expert', route)  22.1 us
    ppermute x9, starting transfers between devices, swap(): return lax.ppermute(block, 'expert', route)  13.8 us
    unnamed x6, local copies, waits for them, and re-layouts  6.11 us
    pallas_call x2, Pallas kernels, load_weights(): pl.pallas_call(load_body, in_specs=[pl.BlockSpec(memory_space=pltpu.HBM)]...  4.99 us
    pallas_call x1, Pallas kernels, expert_rows(): pl.pallas_call(expert_body, grid=(count // tile,), in_specs=[pl.BlockSpec...  3.15 us
  transfers between devices with their start and end apart: 9, of which 5 were waited for; matrix products, arithmetic and copies ran while one was open for 4% of the time, Pallas kernels for 9%

profile of v5, /device:TPU:0, one launch (start us, length us, event | category | flops | bytes accessed | tf_op | source)
XLA Modules:
  0.0 53.8 jit_solution(14168354423144779005)
XLA Ops:
  0.0 0.5 collective-permute-start.2
  0.5 0.0 collective-permute-start.3
  0.5 0.5 collective-permute-start.4
  1.7 0.7 %select_reduce_fusion = f32[16,8]{0,1:T(8,128)S(1)} fusion(f32[16,4]{0,1:T(4,128)} %param.10, s32[16,4]{0,1:T(4,128)} %param.9, pred[16]{0:T(512)(128)(4,1)S(1)} %iota_compare_fusion.1), kind=kLoop, calls=%fused_computation.10 | loop fusion | flops 1920 | bytes 1040 | tf_op jit(solution)/shard_map/reduce_sum | solution.py:42
  2.4 0.1 copy.13
  2.5 0.1 copy.12
  2.5 1.0 %concatenate.15 = bf16[16,3712]{1,0:T(8,128)(2,1)S(1)} concatenate(bf16[16,3584]{1,0:T(8,128)(2,1)} %param.7, bf16[16,8]{1,0:T(8,128)(2,1)S(1)} %get-tuple-element.34, bf16[16,8]{1,0:T(8,128)(2,1)S(1)} %get-tuple-element.33, bf16[16,112]{1,0:T(8,128)(2,1)S(1)} %broadcast_in_dim.22), dimensions={1} | concatenate | bytes 237568 | tf_op jit(solution)/shard_map/concatenate | solution.py:126
  3.5 3.6 %collective-permute-start = (bf16[16,3712]{1,0:T(8,128)(2,1)S(1)}, bf16[16,3712]{1,0:T(8,128)(2,1)S(1)}, u32[]{:S(2)}, u32[]{:S(2)}) collective-permute-start(bf16[16,3712]{1,0:T(8,128)(2,1)S(1)} %concatenate.15), channel_id=1, source_target_pairs={{0,8},{1,3},{2,10},{3,1},{4,12},{5,7},{6,14},{7,5},{8,0},{9,11},{1... | collective-permute-start | bytes 356360 | tf_op jit(solution)/shard_map/ppermute | solution.py:21
  7.1 2.8 %collective-permute-done = bf16[16,3712]{1,0:T(8,128)(2,1)S(1)} collective-permute-done((bf16[16,3712]{1,0:T(8,128)(2,1)S(1)}, bf16[16,3712]{1,0:T(8,128)(2,1)S(1)}, u32[]{:S(2)}, u32[]{:S(2)}) %collective-permute-start) | collective-permute-done | bytes 118816 | tf_op jit(solution)/shard_map/ppermute | solution.py:21
  10.0 2.3 %collective-permute-start.1 = (bf16[32,3712]{1,0:T(8,128)(2,1)S(1)}, bf16[32,3712]{1,0:T(8,128)(2,1)S(1)}, u32[]{:S(2)}, u32[]{:S(2)}) collective-permute-start(bf16[32,3712]{1,0:T(8,128)(2,1)S(1)} %pad_maximum_fusion.2), channel_id=1, source_target_pairs={{0,4},{1,9},{2,6},{3,11},{4,0},{5,13},{6,2},{7,15},{8,12},{9,1},{1... | collective-permute-start | bytes 712712 | tf_op jit(solution)/shard_map/ppermute | solution.py:21
  12.3 0.0 copy-start
  12.3 2.0 %copy-done = bf16[1,3584,512]{2,1,0:T(8,128)(2,1)S(1)} copy-done((bf16[1,3584,512]{2,1,0:T(8,128)(2,1)S(1)}, bf16[1,3584,512]{2,1,0:T(8,128)(2,1)}, u32[]{:S(2)}) %copy-start) | copy-done | bytes 3670040
  14.3 0.0 copy-start.1
  14.3 2.0 %copy-done.1 = bf16[1,3584,512]{2,1,0:T(8,128)(2,1)S(1)} copy-done((bf16[1,3584,512]{2,1,0:T(8,128)(2,1)S(1)}, bf16[1,3584,512]{2,1,0:T(8,128)(2,1)}, u32[]{:S(2)}) %copy-start.1) | copy-done | bytes 3670040
  16.4 0.0 copy-start.2
  16.4 2.0 %copy-done.2 = bf16[1,512,3584]{2,1,0:T(8,128)(2,1)S(1)} copy-done((bf16[1,512,3584]{2,1,0:T(8,128)(2,1)S(1)}, bf16[1,512,3584]{2,1,0:T(8,128)(2,1)}, u32[]{:S(2)}) %copy-start.2) | copy-done | bytes 3670040
  18.4 0.8 %load.2 = (bf16[1,3584,512]{2,1,0:T(8,128)(2,1)S(1)}, bf16[1,3584,512]{2,1,0:T(8,128)(2,1)S(1)}, bf16[1,512,3584]{2,1,0:T(8,128)(2,1)S(1)}) custom-call(bf16[1,3584,512]{2,1,0:T(8,128)(2,1)S(1)} %copy-done, bf16[1,3584,512]{2,1,0:T(8,128)(2,1)S(1)} %copy-done.1, bf16[1,512,3584]{2,1,0:T(8,128)(2,1)S(1)} %copy-done.2), custom_call_target="tpu_custom_call" | custom-call | flops 10000000000 | tf_op jit(solution)/shard_map/load/pallas_call | solution.py:63
  19.2 0.0 collective-permute-done.1
  19.2 0.0 collective-permute-done.2.refs_0_
  19.2 0.0 collective-permute-done.3.refs_1_
  19.3 0.0 collective-permute-done.4.refs_2_
  19.3 1.6 %collective-permute-start.5 = (bf16[64,3712]{1,0:T(8,128)(2,1)S(1)}, bf16[64,3712]{1,0:T(8,128)(2,1)S(1)}, u32[]{:S(2)}, u32[]{:S(2)}) collective-permute-start(bf16[64,3712]{1,0:T(8,128)(2,1)S(1)} %pad_maximum_fusion.1), channel_id=1, source_target_pairs={{0,2},{1,5},{2,0},{3,7},{4,6},{5,1},{6,4},{7,3},{8,10},{9,13},{10,... | collective-permute-start | bytes 1425416 | tf_op jit(solution)/shard_map/ppermute | solution.py:21
  20.8 4.2 %load.3 = (bf16[1,3584,512]{2,1,0:T(8,128)(2,1)S(1)}, bf16[1,3584,512]{2,1,0:T(8,128)(2,1)S(1)}, bf16[1,512,3584]{2,1,0:T(8,128)(2,1)S(1)}) custom-call(bf16[1,3584,512]{2,1,0:T(8,128)(2,1)} %collective-permute-done.2.refs_0_, bf16[1,3584,512]{2,1,0:T(8,128)(2,1)} %collective-permute-done.3.refs_1_, bf16[1,512,3584]{2,1,0:T(8,128)(2,1)} %collective-permute-done.4.refs_2_), custom_call_target="tpu_custom_call" | custom-call | flops 10000000000 | tf_op jit(solution)/shard_map/load/pallas_call | solution.py:63
  25.1 2.9 %collective-permute-done.5 = bf16[64,3712]{1,0:T(8,128)(2,1)S(1)} collective-permute-done((bf16[64,3712]{1,0:T(8,128)(2,1)S(1)}, bf16[64,3712]{1,0:T(8,128)(2,1)S(1)}, u32[]{:S(2)}, u32[]{:S(2)}) %collective-permute-start.5) | collective-permute-done | bytes 475168 | tf_op jit(solution)/shard_map/ppermute | solution.py:21
  28.0 0.1 pad_maximum_fusion.rows
  28.1 3.2 %experts.1 = f32[128,3584]{1,0:T(8,128)S(1)} custom-call(bf16[128,3712]{1,0:T(8,128)(2,1)S(1)} %pad_maximum_fusion.rows, bf16[1,3584,512]{2,1,0:T(8,128)(2,1)S(1)} %get-tuple-element.24.gate_a, bf16[1,3584,512]{2,1,0:T(8,128)(2,1)S(1)} %get-tuple-element.25.up_a, bf16[1,512,3584]{2,1,0:T(8,128)(2,1)S(1)} %get-tuple-element.26.down_a, ...), custom_call_target="tpu_custom_call" | custom-call | tf_op jit(solution)/shard_map/experts/pallas_call | solution.py:104
  31.3 1.6 %collective-permute-start.6 = (bf16[64,3584]{1,0:T(8,128)(2,1)S(1)}, bf16[64,3584]{1,0:T(8,128)(2,1)S(1)}, u32[]{:S(2)}, u32[]{:S(2)}) collective-permute-start(bf16[64,3584]{1,0:T(8,128)(2,1)S(1)} %slice.41), channel_id=1, source_target_pairs={{0,2},{1,5},{2,0},{3,7},{4,6},{5,1},{6,4},{7,3},{8,10},{9,13},{10,... | collective-permute-start | bytes 1376264 | tf_op jit(solution)/shard_map/ppermute | solution.py:21
  32.8 7.0 %collective-permute-done.6 = bf16[64,3584]{1,0:T(8,128)(2,1)S(1)} collective-permute-done((bf16[64,3584]{1,0:T(8,128)(2,1)S(1)}, bf16[64,3584]{1,0:T(8,128)(2,1)S(1)}, u32[]{:S(2)}, u32[]{:S(2)}) %collective-permute-start.6) | collective-permute-done | bytes 458784 | tf_op jit(solution)/shard_map/ppermute | solution.py:21
  39.8 0.1 slice_add_fusion
  39.9 1.0 %collective-permute-start.7 = (bf16[32,3584]{1,0:T(8,128)(2,1)S(1)}, bf16[32,3584]{1,0:T(8,128)(2,1)S(1)}, u32[]{:S(2)}, u32[]{:S(2)}) collective-permute-start(bf16[32,3584]{1,0:T(8,128)(2,1)S(1)} %slice.42), channel_id=1, source_target_pairs={{0,4},{1,9},{2,6},{3,11},{4,0},{5,13},{6,2},{7,15},{8,12},{9,1},{1... | collective-permute-start | bytes 688136 | tf_op jit(solution)/shard_map/ppermute | solution.py:21
  41.0 6.3 %collective-permute-done.7 = bf16[32,3584]{1,0:T(8,128)(2,1)S(1)} collective-permute-done((bf16[32,3584]{1,0:T(8,128)(2,1)S(1)}, bf16[32,3584]{1,0:T(8,128)(2,1)S(1)}, u32[]{:S(2)}, u32[]{:S(2)}) %collective-permute-start.7) | collective-permute-done | bytes 229408 | tf_op jit(solution)/shard_map/ppermute | solution.py:21
  47.3 0.1 slice_add_fusion.1
  47.4 2.7 %collective-permute-start.8 = (bf16[16,3584]{1,0:T(8,128)(2,1)S(1)}, bf16[16,3584]{1,0:T(8,128)(2,1)S(1)}, u32[]{:S(2)}, u32[]{:S(2)}) collective-permute-start(bf16[16,3584]{1,0:T(8,128)(2,1)S(1)} %slice.43), channel_id=1, source_target_pairs={{0,8},{1,3},{2,10},{3,1},{4,12},{5,7},{6,14},{7,5},{8,0},{9,11},{1... | collective-permute-start | bytes 344072 | tf_op jit(solution)/shard_map/ppermute | solution.py:21
  50.1 3.0 %collective-permute-done.8 = bf16[16,3584]{1,0:T(8,128)(2,1)S(1)} collective-permute-done((bf16[16,3584]{1,0:T(8,128)(2,1)S(1)}, bf16[16,3584]{1,0:T(8,128)(2,1)S(1)}, u32[]{:S(2)}, u32[]{:S(2)}) %collective-permute-start.8) | collective-permute-done | bytes 114720 | tf_op jit(solution)/shard_map/ppermute | solution.py:21
  53.2 0.7 %fusion = bf16[16,3584]{1,0:T(8,128)(2,1)} fusion(f32[32,3584]{1,0:T(8,128)S(1)} %slice_add_fusion.1, bf16[16,3584]{1,0:T(8,128)(2,1)S(1)} %collective-permute-done.8), kind=kLoop, calls=%fused_computation.9 | loop fusion | flops 172032 | bytes 458752 | tf_op jit(solution)/shard_map/convert_element_type | solution.py:136
  (9 shorter events, 0.2 us)
Async XLA Ops:
  0.0 19.2 %collective-permute-start.2 = (bf16[1,3584,512]{2,1,0:T(8,128)(2,1)}, bf16[1,3584,512]{2,1,0:T(8,128)(2,1)}, u32[]{:S(2)}, u32[]{:S(2)}) collective-permute-start(bf16[1,3584,512]{2,1,0:T(8,128)(2,1)} %refs_0_), channel_id=1, source_target_pairs={{0,1},{1,0},{2,3},{3,2},{4,5},{5,4},{6,7},{7,6},{8,9},{9,8},{10,11... | collective-permute-start | bytes 11010056 | tf_op jit(solution)/shard_map/ppermute | solution.py:21
  0.5 18.8 %collective-permute-start.3 = (bf16[1,3584,512]{2,1,0:T(8,128)(2,1)}, bf16[1,3584,512]{2,1,0:T(8,128)(2,1)}, u32[]{:S(2)}, u32[]{:S(2)}) collective-permute-start(bf16[1,3584,512]{2,1,0:T(8,128)(2,1)} %refs_1_), channel_id=1, source_target_pairs={{0,1},{1,0},{2,3},{3,2},{4,5},{5,4},{6,7},{7,6},{8,9},{9,8},{10,11... | collective-permute-start | bytes 11010056 | tf_op jit(solution)/shard_map/ppermute | solution.py:21
  0.5 18.7 %collective-permute-start.4 = (bf16[1,512,3584]{2,1,0:T(8,128)(2,1)}, bf16[1,512,3584]{2,1,0:T(8,128)(2,1)}, u32[]{:S(2)}, u32[]{:S(2)}) collective-permute-start(bf16[1,512,3584]{2,1,0:T(8,128)(2,1)} %refs_2_), channel_id=1, source_target_pairs={{0,1},{1,0},{2,3},{3,2},{4,5},{5,4},{6,7},{7,6},{8,9},{9,8},{10,11... | collective-permute-start | bytes 11010056 | tf_op jit(solution)/shard_map/ppermute | solution.py:21
  3.5 6.4 %collective-permute-start = (bf16[16,3712]{1,0:T(8,128)(2,1)S(1)}, bf16[16,3712]{1,0:T(8,128)(2,1)S(1)}, u32[]{:S(2)}, u32[]{:S(2)}) collective-permute-start(bf16[16,3712]{1,0:T(8,128)(2,1)S(1)} %concatenate.15), channel_id=1, source_target_pairs={{0,8},{1,3},{2,10},{3,1},{4,12},{5,7},{6,14},{7,5},{8,0},{9,11},{1... | collective-permute-start | bytes 356360 | tf_op jit(solution)/shard_map/ppermute | solution.py:21
  10.0 9.2 %collective-permute-start.1 = (bf16[32,3712]{1,0:T(8,128)(2,1)S(1)}, bf16[32,3712]{1,0:T(8,128)(2,1)S(1)}, u32[]{:S(2)}, u32[]{:S(2)}) collective-permute-start(bf16[32,3712]{1,0:T(8,128)(2,1)S(1)} %pad_maximum_fusion.2), channel_id=1, source_target_pairs={{0,4},{1,9},{2,6},{3,11},{4,0},{5,13},{6,2},{7,15},{8,12},{9,1},{1... | collective-permute-start | bytes 712712 | tf_op jit(solution)/shard_map/ppermute | solution.py:21
  12.3 2.0 %copy-start = (bf16[1,3584,512]{2,1,0:T(8,128)(2,1)S(1)}, bf16[1,3584,512]{2,1,0:T(8,128)(2,1)}, u32[]{:S(2)}) copy-start(bf16[1,3584,512]{2,1,0:T(8,128)(2,1)} %refs_0_) | copy-start | bytes 11010052
  14.3 2.0 %copy-start.1 = (bf16[1,3584,512]{2,1,0:T(8,128)(2,1)S(1)}, bf16[1,3584,512]{2,1,0:T(8,128)(2,1)}, u32[]{:S(2)}) copy-start(bf16[1,3584,512]{2,1,0:T(8,128)(2,1)} %refs_1_) | copy-start | bytes 11010052
  16.4 2.0 %copy-start.2 = (bf16[1,512,3584]{2,1,0:T(8,128)(2,1)S(1)}, bf16[1,512,3584]{2,1,0:T(8,128)(2,1)}, u32[]{:S(2)}) copy-start(bf16[1,512,3584]{2,1,0:T(8,128)(2,1)} %refs_2_) | copy-start | bytes 11010052
  19.3 8.7 %collective-permute-start.5 = (bf16[64,3712]{1,0:T(8,128)(2,1)S(1)}, bf16[64,3712]{1,0:T(8,128)(2,1)S(1)}, u32[]{:S(2)}, u32[]{:S(2)}) collective-permute-start(bf16[64,3712]{1,0:T(8,128)(2,1)S(1)} %pad_maximum_fusion.1), channel_id=1, source_target_pairs={{0,2},{1,5},{2,0},{3,7},{4,6},{5,1},{6,4},{7,3},{8,10},{9,13},{10,... | collective-permute-start | bytes 1425416 | tf_op jit(solution)/shard_map/ppermute | solution.py:21
  31.3 8.5 %collective-permute-start.6 = (bf16[64,3584]{1,0:T(8,128)(2,1)S(1)}, bf16[64,3584]{1,0:T(8,128)(2,1)S(1)}, u32[]{:S(2)}, u32[]{:S(2)}) collective-permute-start(bf16[64,3584]{1,0:T(8,128)(2,1)S(1)} %slice.41), channel_id=1, source_target_pairs={{0,2},{1,5},{2,0},{3,7},{4,6},{5,1},{6,4},{7,3},{8,10},{9,13},{10,... | collective-permute-start | bytes 1376264 | tf_op jit(solution)/shard_map/ppermute | solution.py:21
  39.9 7.4 %collective-permute-start.7 = (bf16[32,3584]{1,0:T(8,128)(2,1)S(1)}, bf16[32,3584]{1,0:T(8,128)(2,1)S(1)}, u32[]{:S(2)}, u32[]{:S(2)}) collective-permute-start(bf16[32,3584]{1,0:T(8,128)(2,1)S(1)} %slice.42), channel_id=1, source_target_pairs={{0,4},{1,9},{2,6},{3,11},{4,0},{5,13},{6,2},{7,15},{8,12},{9,1},{1... | collective-permute-start | bytes 688136 | tf_op jit(solution)/shard_map/ppermute | solution.py:21
  47.4 5.8 %collective-permute-start.8 = (bf16[16,3584]{1,0:T(8,128)(2,1)S(1)}, bf16[16,3584]{1,0:T(8,128)(2,1)S(1)}, u32[]{:S(2)}, u32[]{:S(2)}) collective-permute-start(bf16[16,3584]{1,0:T(8,128)(2,1)S(1)} %slice.43), channel_id=1, source_target_pairs={{0,8},{1,3},{2,10},{3,1},{4,12},{5,7},{6,14},{7,5},{8,0},{9,11},{1... | collective-permute-start | bytes 344072 | tf_op jit(solution)/shard_map/ppermute | solution.py:21
